TPU v7x, 256 devices: a 2x2x32 block of a 4x8x32 slice. The times are simulated.
256 devices in a mesh: groups: 4 (over x, y), gx: 64 (over z, core).
Axes of the slice: x: 2, y: 2, z: 32, core: 2. Of those that a mesh axis runs over, the one named last changes fastest.
The devices are a block of a 4x8x32 slice.
Arguments:
- velocity: float32 [2, 4096, 512], P(None, ('groups', 'gx')), parts along dimension 1, may hold values from -6 to 6
- cotangent: float32 [2, 4096, 512], P(None, ('groups', 'gx')), parts along dimension 1, may hold values from -6 to 6
- w_first: float32 [3, 3, 32, 2], replicated, may hold values from -1.5 to 1.5
- b_first: float32 [32], replicated, may hold values from -3 to 3
- w_hidden: float32 [2, 3, 3, 32, 32], replicated, may hold values from -0.375 to 0.375
- b_hidden: float32 [2, 32], replicated, may hold values from -3 to 3
- w_last: float32 [3, 3, 2, 32], replicated, may hold values from -0.375 to 0.375
Outputs:
- grad_velocity: float32 [2, 4096, 512], P(None, ('groups', 'gx')), parts along dimension 1
- grad_w_first: float32 [12, 3, 32, 2], P('groups'), parts along dimension 0
- grad_b_first: float32 [128], P('groups'), parts along dimension 0
- grad_w_hidden: float32 [8, 3, 3, 32, 32], P('groups'), parts along dimension 0
- grad_b_hidden: float32 [8, 32], P('groups'), parts along dimension 0
- grad_w_last: float32 [12, 3, 2, 32], P('groups'), parts along dimension 0
- grad_b_last: float32 [8], P('groups'), parts along dimension 0
There are 4 independent parts, one for each index of `groups`. A program takes and returns all parts, laid end to end along the dimension named above; an argument that names none is the same for every part. Nothing has to cross between parts.
All inputs are finite; a program needn't handle non-finite values.
Results may differ from a plain program's by a relative error of at most 0.00012.
Values sent between devices are 32-bit elements; how exact they have to be, the bound alone decides.
No kernel may reach another device: no remote copies, remote signals or barrier semaphores. Data moves between devices by JAX's collectives and lax.ppermute only.
A program may use at most 128 MiB of HBM per device.

v0:
```python
import jax
import jax.numpy as jnp
from jax import lax
from jax.sharding import Mesh
from jax.sharding import PartitionSpec as P

ITERS = 8
GX = ("gx_0", "gx_1")
GROUPS_GX = ("groups", "gx_0", "gx_1")


step_size = 0.25


def padded_2(cells, sides, width):
    for axis, dim in sides:
        count = lax.axis_size(axis)
        head = lax.slice_in_dim(cells, 0, width, axis=dim)
        tail = lax.slice_in_dim(cells, cells.shape[dim] - width, cells.shape[dim], axis=dim)
        cells = jnp.concatenate(
            [
                lax.ppermute(tail, axis, [(i, (i + 1) % count) for i in range(count)]),
                cells,
                lax.ppermute(head, axis, [((i + 1) % count, i) for i in range(count)]),
            ],
            axis=dim,
        )
    return cells


def from_everyone(x, axis):
    length = lax.axis_size(axis)
    return lax.all_to_all(jnp.broadcast_to(x[None], (length, *x.shape)), axis, 0, 0, tiled=True)


def of_everyone(x, axis):
    return from_everyone(x, axis).sum(axis=0)


def packed_total(arrays, axis):
    flat, at, finished = (jnp.concatenate([a.reshape(-1) for a in arrays]), 0, [])
    subtotal = of_everyone(flat, axis)
    for a in arrays:
        finished.append(subtotal[at : at + a.size].reshape(a.shape))
        at += a.size
    return tuple(finished)


def shifted(value, axis, steps):
    count = lax.axis_size(axis)
    pairs = [(source, (source + steps) % count) for source in range(count)]
    return lax.ppermute(value, axis, pairs)


def cut_along(x, dim, length):
    before, after = (x.shape[:dim], x.shape[dim + 1 :])
    return jnp.moveaxis(x.reshape(*before, length, -1, *after), dim, 0)


def sent_and_summed(x, axis, dim):
    length = lax.axis_size(axis)
    parts = lax.all_to_all(cut_along(x, dim, length), axis, 0, 0, tiled=True)
    return jnp.sum(parts, axis=0)


def summed_rows(x, axes, dim):
    far, near = axes
    parts = cut_along(x, dim, lax.axis_size(far))
    nearer = sent_and_summed(parts, near, dim + 1)
    arrived = lax.all_to_all(nearer, far, split_axis=0, concat_axis=0, tiled=True)
    return arrived.sum(axis=0)


def filled_up(lines, length):
    spare = -lines.shape[0] % length
    if not spare:
        return lines
    return jnp.concatenate([lines, jnp.zeros((spare, *lines.shape[1:]), lines.dtype)])


def laid_out(parts, dim):
    parts = jnp.moveaxis(parts, 0, dim)
    dims = parts.shape
    return parts.reshape(*dims[:dim], dims[dim] * dims[dim + 1], *dims[dim + 2 :])


def gathered_by_axis(x, axes, dim):
    far, near = axes
    leading = from_everyone(x, far)
    parts = jnp.swapaxes(from_everyone(leading, near), 0, 1)
    return laid_out(parts.reshape(-1, *x.shape), dim)


def nested_sum(x, axes):
    own = summed_rows(filled_up(x, lax.axis_size(axes[0]) * lax.axis_size(axes[1])), axes, 0)
    whole = gathered_by_axis(own, axes, 0)
    return whole[: len(x)].reshape(x.shape)


def together(arrays, axis):
    flat, at, finished = (jnp.concatenate([a.reshape(-1) for a in arrays]), 0, [])
    subtotal = nested_sum(flat, axis)
    for a in arrays:
        finished.append(subtotal[at : at + a.size].reshape(a.shape))
        at += a.size
    return tuple(finished)


def col_stack(padded):
    return jnp.stack([jnp.roll(padded, 1, axis=2), padded, jnp.roll(padded, -1, axis=2)])


def conv_rows(padded, w, b):
    count = padded.shape[1] - 2
    stacked = col_stack(padded)
    out = b[:, None, None] + jnp.zeros((w.shape[2], count, padded.shape[2]), jnp.float32)
    for p in range(3):
        out = out + jnp.einsum(
            "qok,qkxy->oxy", w[p], stacked[:, :, p : p + count], precision=lax.Precision.HIGHEST
        )
    return out


def conv_back(padded, w):
    count = padded.shape[1] - 2
    stacked = jnp.stack([jnp.roll(padded, -1, axis=2), padded, jnp.roll(padded, 1, axis=2)])
    out = jnp.zeros((w.shape[3], count, padded.shape[2]), jnp.float32)
    for p in range(3):
        out = out + jnp.einsum(
            "qok,qoxy->kxy",
            w[p],
            stacked[:, :, 2 - p : 2 - p + count],
            precision=lax.Precision.HIGHEST,
        )
    return out


def weight_terms(error, padded):
    count = error.shape[1]
    stacked = col_stack(padded)
    rows_of = []
    for p in range(3):
        rows_of.append(
            jnp.einsum(
                "oxy,qkxy->qok",
                error,
                stacked[:, :, p : p + count],
                precision=lax.Precision.HIGHEST,
            )
        )
    return jnp.stack(rows_of)


def error_edge(field):
    return padded_2(field, ((GX, 1),), 1)


def laplace(field):
    padded = padded_2(field, ((GX, 0),), 1)
    return 4.0 * field - padded[2:] - padded[:-2] - jnp.roll(field, 1, 1) - jnp.roll(field, -1, 1)


def two_products(residual, image):
    return packed_total((jnp.sum(residual * residual), jnp.sum(residual * image)), GX)


def solve_pressure(source):
    pressure = jnp.zeros_like(source)
    residual = source
    image = laplace(residual)
    norm_now, product = two_products(residual, image)
    alpha = norm_now / product
    direction, along = (residual, image)
    for step in range(ITERS):
        pressure = pressure + alpha * direction
        residual = residual - alpha * along
        if step + 1 < ITERS:
            image = laplace(residual)
            norm_next, product = two_products(residual, image)
            ratio = norm_next / norm_now
            alpha = norm_next / (product - ratio * norm_next / alpha)
            direction = residual + ratio * direction
            along = image + ratio * along
            norm_now = norm_next
    return pressure


def body(velocity, cotangent, w_first, b_first, w_hidden, b_hidden, w_last):
    rows = velocity.shape[1]
    width = velocity.shape[2]
    layers = w_hidden.shape[0] + 2
    weights = [w_first] + [w_hidden[m] for m in range(layers - 2)] + [w_last]
    biases = [b_first] + [b_hidden[m] for m in range(layers - 2)]
    extended = padded_2(velocity, ((GX, 1),), layers)
    actives = []
    padded_list = [extended[:, layers - 1 : layers + rows + 1]]
    current = extended
    for level in range(layers - 1):
        current = jnp.tanh(conv_rows(current, weights[level], biases[level]))
        offset = layers - 2 - level
        padded_list.append(current[:, offset : offset + rows + 2])
        actives.append(current[:, offset + 1 : offset + 1 + rows])
    vel_pad = padded_list[0]
    first = cotangent[0]
    second = cotangent[1]
    incoming = shifted(first[0:1], GX, -1)
    below = jnp.concatenate([first[1:], incoming], axis=0)
    source = -(below - first + (jnp.roll(second, -1, 1) - second))
    pressure = solve_pressure(source)
    previous = shifted(pressure[-1:], GX, 1)
    above = jnp.concatenate([previous, pressure[:-1]], axis=0)
    slope = jnp.stack([pressure - above, pressure - jnp.roll(pressure, 1, 1)])
    adjoint = cotangent - slope
    along_x = (vel_pad[:, 2:] - vel_pad[:, :-2]) * 0.5
    along_y = (jnp.roll(velocity, -1, 2) - jnp.roll(velocity, 1, 2)) * 0.5
    direct = jnp.stack([jnp.sum(adjoint * along_x, axis=0), jnp.sum(adjoint * along_y, axis=0)])
    flux = padded_2(velocity[0:1] * adjoint, ((GX, 1),), 1)
    flux_x = (flux[:, 2:] - flux[:, :-2]) * 0.5
    cross = velocity[1:2] * adjoint
    flux_y = (jnp.roll(cross, -1, 2) - jnp.roll(cross, 1, 2)) * 0.5
    advective = direct - flux_x - flux_y
    error = step_size * adjoint
    w_terms = [None] * layers
    b_terms = [None] * layers
    for level in reversed(range(layers)):
        w_terms[level] = weight_terms(error, padded_list[level])
        b_terms[level] = jnp.sum(error, axis=(1, 2))
        back = conv_back(error_edge(error), weights[level])
        if level > 0:
            error = back * (1.0 - actives[level - 1] * actives[level - 1])
        else:
            through = back
    grad_velocity = adjoint - step_size * advective + through
    factor = 1.0 / jnp.sqrt(jnp.float32(lax.axis_size(GX) * rows * width))
    hidden_w = jnp.stack(w_terms[1 : layers - 1]) * factor
    hidden_b = jnp.stack(b_terms[1 : layers - 1]) * factor
    totals = together(
        (
            w_terms[0] * factor,
            b_terms[0] * factor,
            hidden_w,
            hidden_b,
            w_terms[layers - 1] * factor,
            b_terms[layers - 1] * factor,
        ),
        ("gx_0", "gx_1"),
    )
    return (grad_velocity, totals[0], totals[1], totals[2], totals[3], totals[4], totals[5])


def solution(mesh):
    finer = Mesh(mesh.devices.reshape(mesh.shape["groups"], 32, 2), ("groups", "gx_0", "gx_1"))
    placed = (P(None, GROUPS_GX, None), P(None, GROUPS_GX, None), P(), P(), P(), P(), P())
    return jax.shard_map(
        body,
        mesh=finer,
        in_specs=placed,
        out_specs=(
            P(None, GROUPS_GX, None),
            P("groups", None, None, None),
            P("groups"),
            P("groups", None, None, None, None),
            P("groups", None),
            P("groups", None, None, None),
            P("groups"),
        ),
        check_vma=False,
    )
```

profile of v0, /device:TPU:37, one launch (start us, length us, event | category | flops | bytes accessed | tf_op | source)
XLA Modules:
  0.0 555.9 jit_solution(17286767472647653708)
XLA Ops:
  4.8 17.3 %collective-permute-start.18 = (f32[2,4,512]{2,0,1:T(2,128)S(1)}, f32[2,4,512]{2,0,1:T(2,128)S(1)}, u32[]{:S(2)}, u32[]{:S(2)}) collective-permute-start(f32[2,4,512]{2,0,1:T(2,128)S(1)} %get-tuple-element.150), channel_id=1, source_target_pairs={{1,0},{2,1},{3,2},{4,3},{5,4},{6,5},{7,6},{8,7},{9,8},{10,9},{11,1... | collective-permute-start | bytes 49160 | tf_op jit(solution)/shard_map/ppermute | solution.py:24
  38.9 14.6 %all-to-all-start = ((f32[64,1,2]{2,1,0:T(1,128)}), f32[64,1,2]{2,1,0:T(1,128)S(1)}, u32[]{:S(2)}, u32[]{:S(2)}) async-start(f32[64,1,2]{2,1,0:T(1,128)} %broadcast_in_dim.22), calls=%async_computation | async-start | bytes 65536 | tf_op jit(solution)/shard_map/all_to_all | solution.py:33
  54.1 21.2 %all-to-all-done = f32[64,1,2]{2,1,0:T(1,128)S(1)} async-done(((f32[64,1,2]{2,1,0:T(1,128)}), f32[64,1,2]{2,1,0:T(1,128)S(1)}, u32[]{:S(2)}, u32[]{:S(2)}) %all-to-all-start) | async-done | bytes 544 | tf_op jit(solution)/shard_map/all_to_all | solution.py:33
  83.1 8.1 %all-to-all-start.1 = ((f32[64,1,2]{2,1,0:T(1,128)}), f32[64,1,2]{2,1,0:T(1,128)S(1)}, u32[]{:S(2)}, u32[]{:S(2)}) async-start(f32[64,1,2]{2,1,0:T(1,128)} %broadcast_in_dim.23), calls=%async_computation.1 | async-start | bytes 65536 | tf_op jit(solution)/shard_map/all_to_all | solution.py:33
  91.9 21.4 %all-to-all-done.1 = f32[64,1,2]{2,1,0:T(1,128)S(1)} async-done(((f32[64,1,2]{2,1,0:T(1,128)}), f32[64,1,2]{2,1,0:T(1,128)S(1)}, u32[]{:S(2)}, u32[]{:S(2)}) %all-to-all-start.1) | async-done | bytes 544 | tf_op jit(solution)/shard_map/all_to_all | solution.py:33
  124.1 8.4 %all-to-all-start.2 = ((f32[64,1,2]{2,1,0:T(1,128)}), f32[64,1,2]{2,1,0:T(1,128)S(1)}, u32[]{:S(2)}, u32[]{:S(2)}) async-start(f32[64,1,2]{2,1,0:T(1,128)} %broadcast_in_dim.24), calls=%async_computation.2 | async-start | bytes 65536 | tf_op jit(solution)/shard_map/all_to_all | solution.py:33
  180.4 23.2 %all-to-all-start.3 = ((f32[64,1,2]{2,1,0:T(1,128)}), f32[64,1,2]{2,1,0:T(1,128)S(1)}, u32[]{:S(2)}, u32[]{:S(2)}) async-start(f32[64,1,2]{2,1,0:T(1,128)} %broadcast_in_dim.25), calls=%async_computation.3 | async-start | bytes 65536 | tf_op jit(solution)/shard_map/all_to_all | solution.py:33
  207.4 18.0 %all-to-all-done.3 = f32[64,1,2]{2,1,0:T(1,128)S(1)} async-done(((f32[64,1,2]{2,1,0:T(1,128)}), f32[64,1,2]{2,1,0:T(1,128)S(1)}, u32[]{:S(2)}, u32[]{:S(2)}) %all-to-all-start.3) | async-done | bytes 544 | tf_op jit(solution)/shard_map/all_to_all | solution.py:33
  238.0 6.3 %all-to-all-start.4 = ((f32[64,1,2]{2,1,0:T(1,128)}), f32[64,1,2]{2,1,0:T(1,128)S(1)}, u32[]{:S(2)}, u32[]{:S(2)}) async-start(f32[64,1,2]{2,1,0:T(1,128)} %broadcast_in_dim.26), calls=%async_computation.4 | async-start | bytes 65536 | tf_op jit(solution)/shard_map/all_to_all | solution.py:33
  247.0 19.0 %all-to-all-done.4 = f32[64,1,2]{2,1,0:T(1,128)S(1)} async-done(((f32[64,1,2]{2,1,0:T(1,128)}), f32[64,1,2]{2,1,0:T(1,128)S(1)}, u32[]{:S(2)}, u32[]{:S(2)}) %all-to-all-start.4) | async-done | bytes 544 | tf_op jit(solution)/shard_map/all_to_all | solution.py:33
  277.4 8.2 %all-to-all-start.5 = ((f32[64,1,2]{2,1,0:T(1,128)}), f32[64,1,2]{2,1,0:T(1,128)S(1)}, u32[]{:S(2)}, u32[]{:S(2)}) async-start(f32[64,1,2]{2,1,0:T(1,128)} %broadcast_in_dim.27), calls=%async_computation.5 | async-start | bytes 65536 | tf_op jit(solution)/shard_map/all_to_all | solution.py:33
  288.2 19.2 %all-to-all-done.5 = f32[64,1,2]{2,1,0:T(1,128)S(1)} async-done(((f32[64,1,2]{2,1,0:T(1,128)}), f32[64,1,2]{2,1,0:T(1,128)S(1)}, u32[]{:S(2)}, u32[]{:S(2)}) %all-to-all-start.5) | async-done | bytes 544 | tf_op jit(solution)/shard_map/all_to_all | solution.py:33
  317.9 8.2 %all-to-all-start.6 = ((f32[64,1,2]{2,1,0:T(1,128)}), f32[64,1,2]{2,1,0:T(1,128)}, u32[]{:S(2)}, u32[]{:S(2)}) async-start(f32[64,1,2]{2,1,0:T(1,128)} %broadcast_in_dim.28), calls=%async_computation.6 | async-start | bytes 65536 | tf_op jit(solution)/shard_map/all_to_all | solution.py:33
  328.8 19.6 %all-to-all-done.6 = f32[64,1,2]{2,1,0:T(1,128)} async-done(((f32[64,1,2]{2,1,0:T(1,128)}), f32[64,1,2]{2,1,0:T(1,128)}, u32[]{:S(2)}, u32[]{:S(2)}) %all-to-all-start.6) | async-done | bytes 544 | tf_op jit(solution)/shard_map/all_to_all | solution.py:33
  360.5 8.4 %all-to-all-start.7 = ((f32[64,1,2]{2,1,0:T(1,128)}), f32[64,1,2]{2,1,0:T(1,128)S(1)}, u32[]{:S(2)}, u32[]{:S(2)}) async-start(f32[64,1,2]{2,1,0:T(1,128)} %broadcast_in_dim.29), calls=%async_computation.7 | async-start | bytes 65536 | tf_op jit(solution)/shard_map/all_to_all | solution.py:33
  371.4 18.8 %all-to-all-done.7 = f32[64,1,2]{2,1,0:T(1,128)S(1)} async-done(((f32[64,1,2]{2,1,0:T(1,128)}), f32[64,1,2]{2,1,0:T(1,128)S(1)}, u32[]{:S(2)}, u32[]{:S(2)}) %all-to-all-start.7) | async-done | bytes 544 | tf_op jit(solution)/shard_map/all_to_all | solution.py:33
  399.5 6.7 %fusion.69 = f32[1,3,2,32]{3,2,1,0:T(2,128)S(1)} fusion(f32[1,32,18,512]{3,1,2,0:T(8,128)} %maximum_bitcast_fusion.15, f32[1,32,18,512]{3,1,2,0:T(8,128)S(1)} %bitcast.494, f32[1,32,18,512]{3,1,2,0:T(8,128)} %maximum_bitcast_fusion.14, f32[2,16,512]{2,0,1:T(2,128)S(1)} %get-tuple-element.68), kind=kOutput, calls=%fused_computation.105 | convolution fusion | flops 20660224 | bytes 3605248 | tf_op jit(solution)/shard_map/oxy,qkxy->qok/dot_general | solution.py:144
  406.2 5.0 fusion.70
  411.1 5.0 fusion.71
  482.5 6.4 %all_to_all.73 = f32[2,32,308]{2,1,0:T(8,128)S(1)} all-to-all(f32[2,32,308]{2,1,0:T(8,128)S(1)} %copy.264), channel_id=1, replica_groups=mesh['groups'=4,'gx_0'=32,'gx_1'=2] {'gx_1'}, dimensions={0} | all-to-all | bytes 157696 | tf_op jit(solution)/shard_map/all_to_all | solution.py:62
  498.5 18.8 %all-to-all-done.9 = f32[32,1,308]{2,1,0:T(1,128)S(1)} async-done(((f32[32,1,308]{2,1,0:T(1,128)}), f32[32,1,308]{2,1,0:T(1,128)S(1)}, u32[]{:S(2)}, u32[]{:S(2)}) %all-to-all-start.9) | async-done | bytes 39456 | tf_op jit(solution)/shard_map/all_to_all | solution.py:70
  518.0 4.8 all-to-all-start.10
  529.8 14.9 %all-to-all-done.10 = f32[32,1,308]{2,1,0:T(1,128)S(1)} async-done(((f32[32,1,308]{2,1,0:T(1,128)}), f32[32,1,308]{2,1,0:T(1,128)S(1)}, u32[]{:S(2)}, u32[]{:S(2)}) %all-to-all-start.10) | async-done | bytes 39456 | tf_op jit(solution)/shard_map/all_to_all | solution.py:33
  544.7 6.3 %all_to_all.74 = f32[2,32,308]{2,1,0:T(8,128)S(1)} all-to-all(f32[2,32,308]{2,1,0:T(8,128)S(1)} %broadcast_in_dim.32), channel_id=1, replica_groups=mesh['groups'=4,'gx_0'=32,'gx_1'=2] {'gx_1'}, dimensions={0} | all-to-all | bytes 157696 | tf_op jit(solution)/shard_map/all_to_all | solution.py:33
  (404 shorter events, 216.7 us)
Async XLA Ops:
  1.6 131.0 %collective-permute-start.19 = (f32[2,4,512]{2,0,1:T(2,128)S(1)}, f32[2,4,512]{2,0,1:T(2,128)S(1)}, u32[]{:S(2)}, u32[]{:S(2)}) collective-permute-start(f32[2,4,512]{2,0,1:T(2,128)S(1)} %get-tuple-element.151), channel_id=1, source_target_pairs={{0,1},{1,2},{2,3},{3,4},{4,5},{5,6},{6,7},{7,8},{8,9},{9,10},{10,1... | collective-permute-start | bytes 49160 | tf_op jit(solution)/shard_map/ppermute | solution.py:22
  4.8 127.9 %collective-permute-start.18 = (f32[2,4,512]{2,0,1:T(2,128)S(1)}, f32[2,4,512]{2,0,1:T(2,128)S(1)}, u32[]{:S(2)}, u32[]{:S(2)}) collective-permute-start(f32[2,4,512]{2,0,1:T(2,128)S(1)} %get-tuple-element.150), channel_id=1, source_target_pairs={{1,0},{2,1},{3,2},{4,3},{5,4},{6,5},{7,6},{8,7},{9,8},{10,9},{11,1... | collective-permute-start | bytes 49160 | tf_op jit(solution)/shard_map/ppermute | solution.py:24
  22.8 9.4 %collective-permute-start = (f32[1,512]{1,0:T(1,128)S(1)}, f32[1,512]{1,0:T(1,128)S(1)}, u32[]{:S(2)}, u32[]{:S(2)}) collective-permute-start(f32[1,512]{1,0:T(1,128)S(1)} %slice_bitcast_fusion.7), channel_id=1, source_target_pairs={{0,63},{1,0},{2,1},{3,2},{4,3},{5,4},{6,5},{7,6},{8,7},{9,8},{10,9... | collective-permute-start | bytes 6152 | tf_op jit(solution)/shard_map/ppermute | solution.py:52
  38.9 36.4 %all-to-all-start = ((f32[64,1,2]{2,1,0:T(1,128)}), f32[64,1,2]{2,1,0:T(1,128)S(1)}, u32[]{:S(2)}, u32[]{:S(2)}) async-start(f32[64,1,2]{2,1,0:T(1,128)} %broadcast_in_dim.22), calls=%async_computation | async-start | bytes 65536 | tf_op jit(solution)/shard_map/all_to_all | solution.py:33
  83.1 30.1 %all-to-all-start.1 = ((f32[64,1,2]{2,1,0:T(1,128)}), f32[64,1,2]{2,1,0:T(1,128)S(1)}, u32[]{:S(2)}, u32[]{:S(2)}) async-start(f32[64,1,2]{2,1,0:T(1,128)} %broadcast_in_dim.23), calls=%async_computation.1 | async-start | bytes 65536 | tf_op jit(solution)/shard_map/all_to_all | solution.py:33
  124.1 44.4 %all-to-all-start.2 = ((f32[64,1,2]{2,1,0:T(1,128)}), f32[64,1,2]{2,1,0:T(1,128)S(1)}, u32[]{:S(2)}, u32[]{:S(2)}) async-start(f32[64,1,2]{2,1,0:T(1,128)} %broadcast_in_dim.24), calls=%async_computation.2 | async-start | bytes 65536 | tf_op jit(solution)/shard_map/all_to_all | solution.py:33
  174.6 3.2 collective-permute-start.8
  180.4 45.0 %all-to-all-start.3 = ((f32[64,1,2]{2,1,0:T(1,128)}), f32[64,1,2]{2,1,0:T(1,128)S(1)}, u32[]{:S(2)}, u32[]{:S(2)}) async-start(f32[64,1,2]{2,1,0:T(1,128)} %broadcast_in_dim.25), calls=%async_computation.3 | async-start | bytes 65536 | tf_op jit(solution)/shard_map/all_to_all | solution.py:33
  232.0 3.3 collective-permute-start.9
  238.0 28.0 %all-to-all-start.4 = ((f32[64,1,2]{2,1,0:T(1,128)}), f32[64,1,2]{2,1,0:T(1,128)S(1)}, u32[]{:S(2)}, u32[]{:S(2)}) async-start(f32[64,1,2]{2,1,0:T(1,128)} %broadcast_in_dim.26), calls=%async_computation.4 | async-start | bytes 65536 | tf_op jit(solution)/shard_map/all_to_all | solution.py:33
  271.5 3.2 collective-permute-start.11
  277.4 30.0 %all-to-all-start.5 = ((f32[64,1,2]{2,1,0:T(1,128)}), f32[64,1,2]{2,1,0:T(1,128)S(1)}, u32[]{:S(2)}, u32[]{:S(2)}) async-start(f32[64,1,2]{2,1,0:T(1,128)} %broadcast_in_dim.27), calls=%async_computation.5 | async-start | bytes 65536 | tf_op jit(solution)/shard_map/all_to_all | solution.py:33
  317.9 30.5 %all-to-all-start.6 = ((f32[64,1,2]{2,1,0:T(1,128)}), f32[64,1,2]{2,1,0:T(1,128)}, u32[]{:S(2)}, u32[]{:S(2)}) async-start(f32[64,1,2]{2,1,0:T(1,128)} %broadcast_in_dim.28), calls=%async_computation.6 | async-start | bytes 65536 | tf_op jit(solution)/shard_map/all_to_all | solution.py:33
  360.5 29.8 %all-to-all-start.7 = ((f32[64,1,2]{2,1,0:T(1,128)}), f32[64,1,2]{2,1,0:T(1,128)S(1)}, u32[]{:S(2)}, u32[]{:S(2)}) async-start(f32[64,1,2]{2,1,0:T(1,128)} %broadcast_in_dim.29), calls=%async_computation.7 | async-start | bytes 65536 | tf_op jit(solution)/shard_map/all_to_all | solution.py:33
  417.9 8.2 %collective-permute-start.22 = (f32[2,1,512]{2,0,1:T(2,128)S(1)}, f32[2,1,512]{2,0,1:T(2,128)S(1)}, u32[]{:S(2)}, u32[]{:S(2)}) collective-permute-start(f32[2,1,512]{2,0,1:T(2,128)S(1)} %get-tuple-element.148), channel_id=1, source_target_pairs={{0,1},{1,2},{2,3},{3,4},{4,5},{5,6},{6,7},{7,8},{8,9},{9,10},{10,1... | collective-permute-start | bytes 12296 | tf_op jit(solution)/shard_map/ppermute | solution.py:22
  419.7 6.4 %collective-permute-start.23 = (f32[2,1,512]{2,0,1:T(2,128)S(1)}, f32[2,1,512]{2,0,1:T(2,128)S(1)}, u32[]{:S(2)}, u32[]{:S(2)}) collective-permute-start(f32[2,1,512]{2,0,1:T(2,128)S(1)} %get-tuple-element.149), channel_id=1, source_target_pairs={{1,0},{2,1},{3,2},{4,3},{5,4},{6,5},{7,6},{8,7},{9,8},{10,9},{11,1... | collective-permute-start | bytes 12296 | tf_op jit(solution)/shard_map/ppermute | solution.py:24
  421.9 104.7 %collective-permute-start.20 = (f32[2,1,512]{2,0,1:T(2,128)}, f32[2,1,512]{2,0,1:T(2,128)}, u32[]{:S(2)}, u32[]{:S(2)}) collective-permute-start(f32[2,1,512]{2,0,1:T(2,128)} %get-tuple-element.137), channel_id=1, source_target_pairs={{1,0},{2,1},{3,2},{4,3},{5,4},{6,5},{7,6},{8,7},{9,8},{10,9},{11,1... | collective-permute-start | bytes 12296 | tf_op jit(solution)/shard_map/ppermute | solution.py:24
  424.8 101.8 %collective-permute-start.21 = (f32[2,1,512]{2,0,1:T(2,128)S(1)}, f32[2,1,512]{2,0,1:T(2,128)}, u32[]{:S(2)}, u32[]{:S(2)}) collective-permute-start(f32[2,1,512]{2,0,1:T(2,128)S(1)} %get-tuple-element.138), channel_id=1, source_target_pairs={{0,1},{1,2},{2,3},{3,4},{4,5},{5,6},{6,7},{7,8},{8,9},{9,10},{10,1... | collective-permute-start | bytes 12296 | tf_op jit(solution)/shard_map/ppermute | solution.py:22
  439.2 3.7 collective-permute-start.25
  462.1 3.9 collective-permute-start.27
  478.9 15.5 %collective-permute-start.28 = (f32[32,1,512]{2,0,1:T(8,128)S(1)}, f32[32,1,512]{2,0,1:T(8,128)S(1)}, u32[]{:S(2)}, u32[]{:S(2)}) collective-permute-start(f32[32,1,512]{2,0,1:T(8,128)S(1)} %get-tuple-element.117), channel_id=1, source_target_pairs={{0,1},{1,2},{2,3},{3,4},{4,5},{5,6},{6,7},{7,8},{8,9},{9,10},{10,1... | collective-permute-start | bytes 196616 | tf_op jit(solution)/shard_map/ppermute | solution.py:22
  479.0 15.4 %collective-permute-start.29 = (f32[32,1,512]{2,0,1:T(8,128)S(1)}, f32[32,1,512]{2,0,1:T(8,128)S(1)}, u32[]{:S(2)}, u32[]{:S(2)}) collective-permute-start(f32[32,1,512]{2,0,1:T(8,128)S(1)} %get-tuple-element.118), channel_id=1, source_target_pairs={{1,0},{2,1},{3,2},{4,3},{5,4},{6,5},{7,6},{8,7},{9,8},{10,9},{11,1... | collective-permute-start | bytes 196616 | tf_op jit(solution)/shard_map/ppermute | solution.py:24
  489.6 27.7 %all-to-all-start.9 = ((f32[32,1,308]{2,1,0:T(1,128)}), f32[32,1,308]{2,1,0:T(1,128)S(1)}, u32[]{:S(2)}, u32[]{:S(2)}) async-start(f32[32,1,308]{2,1,0:T(1,128)} %all_to_all.57), calls=%async_computation.9 | async-start | bytes 98304 | tf_op jit(solution)/shard_map/all_to_all | solution.py:70
  518.0 26.7 %all-to-all-start.10 = ((f32[32,1,308]{2,1,0:T(1,128)}), f32[32,1,308]{2,1,0:T(1,128)S(1)}, u32[]{:S(2)}, u32[]{:S(2)}) async-start(f32[32,1,308]{2,1,0:T(1,128)} %broadcast_in_dim.30), calls=%async_computation.10 | async-start | bytes 98304 | tf_op jit(solution)/shard_map/all_to_all | solution.py:33
  (73 other events, 565.4 us)
where the time goes:
time: 563 us; the launch traced here: 556 us
  waiting for transfers between devices  189 us (34%)
  starting transfers between devices  146 us (26%)
  matrix products  80.3 us (14%)
  local copies, waits for them, and re-layouts  53.3 us (9%)
  other arithmetic  42.3 us (8%)
  between operations  31.7 us (6%)
  blocking collectives  12.6 us (2%)
    all_to_all x9, waiting for transfers between devices, from_everyone(): lax.all_to_all(jnp.broadcast_to(x[None], (length, *x.shape)), axis, 0, 0,...  152 us
    all_to_all x9, starting transfers between devices, from_everyone(): lax.all_to_all(jnp.broadcast_to(x[None], (length, *x.shape)), axis, 0, 0,...  90.1 us
    dot_general x12, matrix products, weight_terms(): jnp.einsum('oxy,qkxy->qok', error, stacked[:, :, p:p + count], precision=...  37.6 us
    ppermute x14, starting transfers between devices, padded_2(): lax.ppermute(head, axis, [((i + 1) % count, i) for i in range(count)])  35.8 us
    dot_general x12, matrix products, conv_back(): jnp.einsum('qok,qoxy->kxy', w[p], stacked[:, :, 2 - p:2 - p + count], pre...  23.9 us
    dot_general x9, matrix products, conv_rows(): jnp.einsum('qok,qkxy->oxy', w[p], stacked[:, :, p:p + count], precision=l...  18.8 us
    all_to_all x1, waiting for transfers between devices, summed_rows(): lax.all_to_all(nearer, far, split_axis=0, concat_axis=0, tiled=True)  18.8 us
    another operation x10, other arithmetic, col_stack(): jnp.stack([jnp.roll(padded, 1, axis=2), padded, jnp.roll(padded, -1, axis...  16.9 us
  transfers between devices with their start and end apart: 40, of which 23 were waited for; matrix products, arithmetic and copies ran while one was open for 23% of the time, Pallas kernels for 0%

commit v1 on v0

v1 whole, which is shorter than its diff:
```python
import functools

import jax
import jax.numpy as jnp
from jax import lax
from jax.experimental import pallas as pl
from jax.experimental.pallas import tpu as pltpu
from jax.sharding import Mesh
from jax.sharding import PartitionSpec as P

ITERS = 8
GX = ("gx_0", "gx_1")
GROUPS_GX = ("groups", "gx_0", "gx_1")
SPREAD_LIMIT = 3000.0
BLOCK = 6
SPAN = BLOCK + 2
F32 = jnp.float32
BF16 = jnp.bfloat16

step_size = 0.25


def from_everyone(x, axis):
    length = lax.axis_size(axis)
    return lax.all_to_all(jnp.broadcast_to(x[None], (length, *x.shape)), axis, 0, 0, tiled=True)


def shifted(value, axis, steps):
    count = lax.axis_size(axis)
    pairs = [(source, (source + steps) % count) for source in range(count)]
    return lax.ppermute(value, axis, pairs)


def turn(x, steps, axis):
    return pltpu.roll(x, steps % x.shape[axis], axis)


def halves(x):
    high = x.astype(BF16)
    return high, (x - high.astype(F32)).astype(BF16)


def starts(first, count):
    return [min(first + BLOCK * i, first + count - BLOCK) for i in range(-(-count // BLOCK))]


def fold_lanes(x):
    total = x[:, :128]
    for at in range(128, x.shape[1], 128):
        total = total + x[:, at : at + 128]
    return total


def lane_groups_summed(x):
    x = fold_lanes(x)
    x = x + turn(x, 64, 1)
    return x + turn(x, 32, 1)


def neighbours(t):
    return turn(t, 1, 0) + turn(t, -1, 0) + turn(t, 1, 1) + turn(t, -1, 1)


def basis_kernel(prev, own, later, basis, sums):
    rows = own.shape[1]
    first = jnp.concatenate([prev[0], own[0], later[0]], axis=0)
    second = jnp.concatenate([prev[1], own[1], later[1]], axis=0)
    source = -(turn(first, -1, 0) - first + (turn(second, -1, 1) - second))
    line = lax.broadcasted_iota(jnp.int32, (2 * ITERS, 128), 0)
    lane = lax.broadcasted_iota(jnp.int32, (2 * ITERS, 128), 1)
    squares, crosses = [], []

    def product(a, b):
        return fold_lanes(jnp.sum(a[rows : 2 * rows] * b[rows : 2 * rows], axis=0, keepdims=True))

    before, now = None, source
    for k in range(ITERS):
        basis[k] = now[rows - 8 : 2 * rows + 8]
        if k == 0:
            after = -0.25 * neighbours(now)
        else:
            after = -0.5 * neighbours(now) - before
        squares.append(product(now, now))
        crosses.append(product(now, after))
        before, now = now, after
    stacked = jnp.concatenate(squares + crosses, axis=0)
    column = jnp.sum(stacked, axis=1, keepdims=True)
    row = jnp.sum(jnp.where(line == lane, column, 0.0), axis=0, keepdims=True)
    sums[...] = jnp.broadcast_to(row, sums.shape)


def quadratic(a, b, mu):
    total = None
    for i, left in enumerate(a):
        inner = None
        for j, right in enumerate(b):
            term = right * mu[i][j]
            inner = term if inner is None else inner + term
        total = left * inner if total is None else total + left * inner
    return total


def spread(a):
    total = jnp.abs(a[0])
    for item in a[1:]:
        total = total + jnp.abs(item)
    return total


def image_of(c):
    out = [4.0 * item for item in c] + [jnp.zeros_like(c[0])]
    out[1] = out[1] + 4.0 * c[0]
    for k in range(1, len(c)):
        out[k + 1] = out[k + 1] + 2.0 * c[k]
        out[k - 1] = out[k - 1] + 2.0 * c[k]
    return out


def combined(factor, a, b):
    out = []
    for k in range(max(len(a), len(b))):
        if k >= len(a):
            out.append(b[k])
        elif k >= len(b):
            out.append(factor * a[k])
        else:
            out.append(b[k] + factor * a[k])
    return out


def pressure_kernel(gathered, basis, pressure, unsafe):
    total = jnp.sum(gathered[...], axis=0, keepdims=True)
    lane = lax.broadcasted_iota(jnp.int32, (1, 128), 1)
    items = [
        jnp.broadcast_to(jnp.sum(jnp.where(lane == k, total, 0.0), axis=1, keepdims=True), (1, 128))
        for k in range(2 * ITERS)
    ]
    moments = [items[0], items[ITERS]]
    for k in range(1, ITERS):
        moments.append(2.0 * items[k] - items[0])
        moments.append(2.0 * items[ITERS + k] - items[ITERS])
    mu = [
        [0.5 * (moments[i + j] + moments[abs(i - j)]) for j in range(min(ITERS + 1, 2 * ITERS - i))]
        for i in range(ITERS)
    ]
    one = jnp.ones((1, 128), F32)
    residual, direction, answer = [one], [one], [jnp.zeros((1, 128), F32)]
    norm_now = items[0]
    safe = norm_now > 0.0
    for step in range(ITERS):
        image = image_of(direction)
        product = quadratic(direction, image, mu)
        bound = spread(direction) * spread(image) * items[0]
        safe = safe & (product > 0.0) & (bound < SPREAD_LIMIT * product)
        alpha = norm_now / product
        answer = combined(alpha, direction, answer)
        if step + 1 < ITERS:
            residual = combined(-alpha, image, residual)
            norm_next = quadratic(residual, residual, mu)
            size = spread(residual)
            safe = safe & (norm_next > 0.0) & (size * size * items[0] < SPREAD_LIMIT * norm_next)
            direction = combined(norm_next / norm_now, direction, residual)
            norm_now = norm_next
    wide = basis.shape[2] // 128
    lam = None
    for k in range(ITERS):
        term = jnp.concatenate([answer[k]] * wide, axis=1) * basis[k]
        lam = term if lam is None else lam + term
    pressure[...] = lam
    unsafe[...] = jnp.where(safe, 0, 1).astype(jnp.int32)


def laplace(field):
    above = shifted(field[-1:], GX, 1)
    below = shifted(field[:1], GX, -1)
    up = jnp.concatenate([above, field[:-1]], axis=0)
    down = jnp.concatenate([field[1:], below], axis=0)
    return 4.0 * field - up - down - jnp.roll(field, 1, 1) - jnp.roll(field, -1, 1)


def sum_of(a, b):
    local = jnp.broadcast_to(jnp.sum(a * b), (1, 128))
    return jnp.sum(from_everyone(local, GX)[:, 0, 0])


def stepwise_pressure(cotangent, later):
    first, second = cotangent[0], cotangent[1]
    below = jnp.concatenate([first[1:], later[0, :1]], axis=0)
    source = -(below - first + (jnp.roll(second, -1, 1) - second))

    def iterate(_, carry):
        pressure, residual, direction, norm_now = carry
        image = laplace(direction)
        alpha = norm_now / sum_of(direction, image)
        pressure = pressure + alpha * direction
        residual = residual - alpha * image
        norm_next = sum_of(residual, residual)
        direction = residual + norm_next / norm_now * direction
        return pressure, residual, direction, norm_next

    start = (jnp.zeros_like(source), source, source, sum_of(source, source))
    pressure = lax.fori_loop(0, ITERS, iterate, start)[0]
    above = shifted(pressure[-8:], GX, 1)
    under = shifted(pressure[:8], GX, -1)
    return jnp.concatenate([above, pressure, under], axis=0)


def banded(taps):
    rows = jnp.concatenate([taps] + [turn(taps, 32 * r, 1) for r in range(1, BLOCK)], axis=0)
    high, low = halves(rows)
    return jnp.concatenate([high, high, low], axis=1)


def banded_narrow(taps):
    rows = jnp.concatenate([taps] + [turn(taps, r, 1) for r in range(1, BLOCK)], axis=0)
    high = rows.astype(BF16).astype(F32)
    low = rows - high
    return (high + turn(high, 16, 1) + turn(low, 32, 1)).astype(BF16)[:, :48]


def banded_out(taps, rows):
    width = (rows + 2) * 32
    padded = -(-width // 128)
    lane = lax.broadcasted_iota(jnp.int32, (rows, padded * 128), 1) // 32
    row = lax.broadcasted_iota(jnp.int32, (rows, padded * 128), 0)
    pieces = []
    for j in range(6):
        piece = jnp.zeros((rows, padded * 128), F32)
        for p in range(3):
            line = jnp.concatenate([taps[p][j : j + 1]] * padded, axis=1)
            piece = piece + jnp.where(lane == row + p, line, 0.0)
        pieces.append(piece)
    return halves(jnp.concatenate(pieces, axis=0))


def side_sum(y):
    n = y.shape[1] // 3
    return turn(y[:, :n], 1, 2) + y[:, n : 2 * n] + turn(y[:, 2 * n :], -1, 2)


def wide_conv(weights, high, low):
    x = jnp.concatenate([high, low, high], axis=0)
    y = jnp.dot(weights, x, preferred_element_type=F32)
    return side_sum(y.reshape(BLOCK, 96, y.shape[1]))


def narrow_conv(weights, pair):
    high, low = halves(jnp.concatenate(pair, axis=0))
    x = jnp.concatenate([high, low, high], axis=0)
    y = jnp.dot(weights, x, preferred_element_type=F32)
    return side_sum(y.reshape(BLOCK, 96, y.shape[1]))


def put(refs, at, value):
    high, low = halves(value.reshape(value.shape[0] * 32, value.shape[2]))
    span = pl.ds(at * 32, value.shape[0] * 32)
    refs[0][span, :] = high
    refs[1][span, :] = low


def take(refs, at, rows):
    span = pl.ds(at * 32, rows * 32)
    return refs[0][span, :], refs[1][span, :]


def forward_kernel(
    prev, own, later, narrow, wide, bias, a0h, a0l, a1h, a1l, a2h, a2l, weights0, weights1, weights2
):
    rows, width = own.shape[1], own.shape[2]
    v = [jnp.concatenate([prev[c, rows - 8 :], own[c], later[c, :8]], axis=0) for c in range(2)]
    weights0[...] = banded_narrow(narrow[...])
    weights1[...] = banded(wide[0])
    weights2[...] = banded(wide[1])
    shift = [jnp.concatenate([bias[m]] * (width // 128), axis=1) for m in range(3)]
    for s in starts(-5, rows + 10):
        pair = [v[c][s + 7 : s + 7 + SPAN] for c in range(2)]
        put((a0h, a0l), s + 5, jnp.tanh(narrow_conv(weights0[...], pair) + shift[0]))
    for s in starts(-4, rows + 8):
        x = take((a0h, a0l), s + 4, SPAN)
        put((a1h, a1l), s + 4, jnp.tanh(wide_conv(weights1[...], *x) + shift[1]))
    for s in starts(-3, rows + 6):
        x = take((a1h, a1l), s + 3, SPAN)
        put((a2h, a2l), s + 3, jnp.tanh(wide_conv(weights2[...], *x) + shift[2]))


def dot_nt(a, b):
    return lax.dot_general(a, b, (((1,), (1,)), ((), ())), preferred_element_type=F32)


def sided(e, axis):
    return jnp.concatenate([turn(e, -1, e.ndim - 1), e, turn(e, 1, e.ndim - 1)], axis=axis)


def wide_terms(err, err_at, act, act_at, rows):
    total = None
    lines = -(-rows // BLOCK)
    for i in range(lines):
        s = min(BLOCK * i, rows - BLOCK)
        e = err[pl.ds((err_at + s) * 32, BLOCK * 32), :].reshape(BLOCK, 32, -1)
        spent = BLOCK * i - s
        if spent:
            e = jnp.concatenate([jnp.zeros_like(e[:spent]), e[spent:]], axis=0)
        high, low = halves(sided(e, 1).reshape(BLOCK * 96, -1))
        ah, al = take(act, act_at + s - 1, SPAN)
        term = dot_nt(
            jnp.concatenate([high, high, low], axis=1), jnp.concatenate([ah, al, ah], axis=1)
        )
        total = term if total is None else total + term
    total = total.reshape(BLOCK, 96, SPAN * 32)
    out = None
    for r in range(BLOCK):
        piece = turn(total[r], -32 * r, 1)[:, :128]
        out = piece if out is None else out + piece
    return out


def eight_rows(x):
    missing = 8 - x.shape[0]
    if not missing:
        return x
    return jnp.concatenate([x, jnp.zeros((missing, x.shape[1]), x.dtype)], axis=0)


def bias_line(err, err_at, rows):
    e = err[pl.ds(err_at * 32, rows * 32), :].reshape(rows, 32, -1)
    column = jnp.sum(fold_lanes(jnp.sum(e, axis=0)), axis=1, keepdims=True)
    line = lax.broadcasted_iota(jnp.int32, (32, 128), 0)
    lane = lax.broadcasted_iota(jnp.int32, (32, 128), 1)
    return eight_rows(jnp.sum(jnp.where(lane == line + 96, column, 0.0), axis=0, keepdims=True))


def backward_kernel(
    factor,
    pressure,
    cprev,
    cown,
    clater,
    vprev,
    vown,
    vlater,
    a0h,
    a0l,
    a1h,
    a1l,
    a2h,
    a2l,
    narrow,
    wide,
    out_taps,
    grad_velocity,
    terms,
    e2,
    e1,
    e0,
    eh,
    el,
    weights,
    weights_narrow,
):
    rows, width = vown.shape[1], vown.shape[2]
    a0, a1, a2, split = (a0h, a0l), (a1h, a1l), (a2h, a2l), (eh, el)

    def extended(prev, own, later, c):
        return jnp.concatenate([prev[c, rows - 8 :], own[c], later[c, :8]], axis=0)

    lam = pressure[...]
    adjoint = [
        extended(cprev, cown, clater, 0) - (lam - turn(lam, 1, 0)),
        extended(cprev, cown, clater, 1) - (lam - turn(lam, 1, 1)),
    ]
    v = [extended(vprev, vown, vlater, c) for c in range(2)]
    e3 = [step_size * item for item in adjoint]

    def slope_of(act, at):
        high, low = take(act, at, BLOCK)
        a = high.astype(F32) + low.astype(F32)
        return (1.0 - a * a).reshape(BLOCK, 32, width)

    def keep(ref, at, value):
        put(split, at, value)
        ref[pl.ds(at * 32, BLOCK * 32), :] = value.reshape(BLOCK * 32, width)

    weights_narrow[...] = banded_narrow(narrow[...])
    for s in starts(-3, rows + 6):
        pair = [e3[c][s + 7 : s + 7 + SPAN] for c in range(2)]
        keep(e2, s + 3, narrow_conv(weights_narrow[...], pair) * slope_of(a2, s + 3))
    weights[...] = banded(wide[1])
    for s in starts(-2, rows + 4):
        x = take(split, s + 2, SPAN)
        e1[pl.ds((s + 2) * 32, BLOCK * 32), :] = (
            wide_conv(weights[...], *x) * slope_of(a1, s + 4)
        ).reshape(BLOCK * 32, width)
    split_rows = (rows + 4) * 32
    high, low = halves(e1[...])
    eh[0:split_rows, :] = high
    el[0:split_rows, :] = low
    weights[...] = banded(wide[0])
    for s in starts(-1, rows + 2):
        x = take(split, s + 1, SPAN)
        e0[pl.ds((s + 1) * 32, BLOCK * 32), :] = (
            wide_conv(weights[...], *x) * slope_of(a0, s + 5)
        ).reshape(BLOCK * 32, width)

    own = slice(8, 8 + rows)
    wh, wl = banded_out(out_taps, rows)
    high, low = halves(e0[...])
    cells = (rows + 2) * 32
    wh, wl = wh[:, :cells], wl[:, :cells]
    y = (
        jnp.dot(wh, high, preferred_element_type=F32)
        + jnp.dot(wh, low, preferred_element_type=F32)
        + jnp.dot(wl, high, preferred_element_type=F32)
    )
    through = []
    for c in range(2):
        parts = [y[(2 * q + c) * rows : (2 * q + c + 1) * rows] for q in range(3)]
        through.append(turn(parts[0], 1, 1) + parts[1] + turn(parts[2], -1, 1))

    cross = []
    for k in range(2):
        flux = v[0] * adjoint[k]
        side = v[1][own] * adjoint[k][own]
        cross.append(
            ((turn(flux, -1, 0) - turn(flux, 1, 0)) * 0.5)[own]
            + (turn(side, -1, 1) - turn(side, 1, 1)) * 0.5
        )
    along_x = [((turn(f, -1, 0) - turn(f, 1, 0)) * 0.5)[own] for f in v]
    along_y = [(turn(f[own], -1, 1) - turn(f[own], 1, 1)) * 0.5 for f in v]
    direct = [
        adjoint[0][own] * along_x[0] + adjoint[1][own] * along_x[1],
        adjoint[0][own] * along_y[0] + adjoint[1][own] * along_y[1],
    ]
    for k in range(2):
        grad_velocity[k] = adjoint[k][own] - step_size * (direct[k] - cross[k]) + through[k]

    scale = factor[0, 0]
    middle1 = wide_terms(e2, 3, a1, 4, rows)
    middle0 = wide_terms(e1, 2, a0, 5, rows)

    outer = jnp.concatenate([sided(e3[c][own], 0) for c in range(2)], axis=0)
    lh, ll = halves(outer)
    ah, al = take(a2, 2, rows + 4)
    last = dot_nt(lh, ah) + dot_nt(lh, al) + dot_nt(ll, ah)
    last = last.reshape(6, rows, (rows + 4) * 32)
    group = lax.broadcasted_iota(jnp.int32, (rows, (rows + 4) * 32), 1) // 32
    line = lax.broadcasted_iota(jnp.int32, (rows, (rows + 4) * 32), 0)
    spare = []
    for p in range(3):
        picked = jnp.sum(jnp.where((group == line + p)[None], last, 0.0), axis=1)
        spare.append(eight_rows(lane_groups_summed(picked)))

    inner = jnp.concatenate(
        [jnp.concatenate([turn(f, 1, 1), f, turn(f, -1, 1)], axis=0) for f in v], axis=0
    )
    lh, ll = halves(inner)
    eh0, el0 = high[32 : 32 + rows * 32], low[32 : 32 + rows * 32]
    begin = dot_nt(lh, eh0) + dot_nt(lh, el0) + dot_nt(ll, eh0)
    tall = rows + 16
    begin = begin.reshape(6, tall, rows * 32)
    group = lax.broadcasted_iota(jnp.int32, (tall, rows * 32), 1) // 32
    line = lax.broadcasted_iota(jnp.int32, (tall, rows * 32), 0)
    for p in range(3):
        picked = jnp.sum(jnp.where((line == group + p + 7)[None], begin, 0.0), axis=1)
        spare.append(eight_rows(lane_groups_summed(picked)))

    spare.append(bias_line(e2, 3, rows))
    spare.append(bias_line(e1, 2, rows))
    spare.append(bias_line(e0, 1, rows))
    lane = lax.broadcasted_iota(jnp.int32, (1, 128), 1)
    ends = jnp.zeros((1, 128), F32)
    for c in range(2):
        end = jnp.sum(jnp.sum(e3[c][own], axis=0, keepdims=True), axis=1, keepdims=True)
        ends = ends + jnp.where(lane == 96 + c, end, 0.0)
    spare.append(eight_rows(ends))
    spare.append(jnp.zeros((96 - 8 * len(spare), 128), F32))
    spare = jnp.concatenate(spare, axis=0)
    kept = lax.broadcasted_iota(jnp.int32, (96, 128), 1) < 96
    terms[0:96, :] = jnp.where(kept, middle1, spare) * scale
    terms[96:192, :] = jnp.where(kept, middle0, 0.0) * scale


def total_of(packed):
    far, near = lax.axis_size("gx_0"), lax.axis_size("gx_1")
    lines, lanes = packed.shape
    half = lax.all_to_all(packed.reshape(near, lines // near, lanes), "gx_1", 0, 0, tiled=True)
    half = half.sum(axis=0)
    part = lax.all_to_all(half.reshape(far, -1, lanes), "gx_0", 0, 0, tiled=True).sum(axis=0)
    half = from_everyone(part, "gx_0").reshape(lines // near, lanes)
    return from_everyone(half, "gx_1").reshape(lines, lanes)


def forward_taps(w):
    out, into = w.shape[2], w.shape[3]
    return jnp.transpose(w, (1, 2, 0, 3)).reshape(3 * out, 3 * into)


def backward_taps(w):
    out, into = w.shape[2], w.shape[3]
    return jnp.transpose(w[::-1, ::-1], (1, 3, 0, 2)).reshape(3 * into, 3 * out)


def narrow_taps(w):
    t = jnp.transpose(w, (1, 2, 3, 0)).reshape(3 * w.shape[2], 2, 3)
    t = jnp.pad(t, ((0, 0), (0, 0), (0, 5))).reshape(-1, 16)
    return jnp.pad(t, ((0, 0), (0, 112)))


def out_taps_of(w):
    t = jnp.pad(w.reshape(3, 6, w.shape[3]), ((0, 0), (0, 2), (0, 0)))
    return jnp.concatenate([t] * 4, axis=2)


def flipped(w):
    return jnp.swapaxes(w[::-1, ::-1], 2, 3)


def shape_of(*dims, dtype=F32):
    return jax.ShapeDtypeStruct(dims, dtype)


def call(kernel, out_shape, scratch=(), **extra):
    return pl.pallas_call(
        kernel,
        out_shape=out_shape,
        scratch_shapes=list(scratch),
        compiler_params=pltpu.CompilerParams(vmem_limit_bytes=60 * 1024 * 1024),
        **extra,
    )


def body(velocity, cotangent, w_first, b_first, w_hidden, b_hidden, w_last):
    rows, width = velocity.shape[1], velocity.shape[2]
    members = lax.axis_size(GX)
    cprev, clater = shifted(cotangent, GX, 1), shifted(cotangent, GX, -1)
    vprev, vlater = shifted(velocity, GX, 1), shifted(velocity, GX, -1)

    wide_pad = ((0, 0), (0, 256 - 96))
    wide = jnp.stack([jnp.pad(forward_taps(w_hidden[m]), wide_pad) for m in range(2)])
    wide_back = jnp.stack([jnp.pad(backward_taps(w_hidden[m]), wide_pad) for m in range(2)])
    narrow = narrow_taps(w_first)
    narrow_back = narrow_taps(flipped(w_last))
    out_taps = out_taps_of(flipped(w_first))
    biases = jnp.stack([b_first, b_hidden[0], b_hidden[1]])
    biases = jnp.broadcast_to(biases[:, :, None], (3, biases.shape[1], 128))

    basis, sums = call(
        basis_kernel, (shape_of(ITERS, rows + 16, width), shape_of(members, 128))
    )(cprev, cotangent, clater)
    gathered = lax.all_to_all(sums.reshape(members, 1, 128), GX, 0, 0, tiled=True)

    heights = (rows + 10, rows + 8, rows + 6)
    held = [shape_of(h * 32, width, dtype=BF16) for h in heights for _ in range(2)]
    actives = call(
        forward_kernel,
        tuple(held),
        [
            pltpu.VMEM((96 * BLOCK, 48), BF16),
            pltpu.VMEM((96 * BLOCK, 3 * SPAN * 32), BF16),
            pltpu.VMEM((96 * BLOCK, 3 * SPAN * 32), BF16),
        ],
    )(vprev, velocity, vlater, narrow, wide, biases)

    quick, unsafe = call(
        pressure_kernel, (shape_of(rows + 16, width), shape_of(1, 128, dtype=jnp.int32))
    )(gathered.reshape(members, 128), basis)
    pressure = lax.cond(
        unsafe[0, 0] != 0,
        lambda c, l, _: stepwise_pressure(c, l),
        lambda c, l, q: q,
        cotangent,
        clater,
        quick,
    )

    factor = 1.0 / jnp.sqrt(jnp.float32(members * rows * width))
    whole = pl.BlockSpec(memory_space=pltpu.VMEM)
    grad_velocity, terms = call(
        backward_kernel,
        (shape_of(2, rows, width), shape_of(192, 128)),
        [
            pltpu.VMEM(((rows + 6) * 32, width), F32),
            pltpu.VMEM(((rows + 4) * 32, width), F32),
            pltpu.VMEM(((rows + 2) * 32, width), F32),
            pltpu.VMEM(((rows + 6) * 32, width), BF16),
            pltpu.VMEM(((rows + 6) * 32, width), BF16),
            pltpu.VMEM((96 * BLOCK, 3 * SPAN * 32), BF16),
            pltpu.VMEM((96 * BLOCK, 48), BF16),
        ],
        in_specs=[pl.BlockSpec(memory_space=pltpu.SMEM)] + [whole] * 16,
    )(
        factor.reshape(1, 1),
        pressure,
        cprev,
        cotangent,
        clater,
        vprev,
        velocity,
        vlater,
        *actives,
        narrow_back,
        wide_back,
        out_taps,
    )
    total = total_of(terms)

    def square(block):
        return jnp.transpose(block.reshape(3, 32, 3, 32), (2, 0, 1, 3))

    spare = total[:96, 96:]
    grad_hidden = jnp.stack([square(total[96:, :96]), square(total[:96, :96])])
    last = spare[:24].reshape(3, 8, 32)[:, :6]
    grad_last = jnp.swapaxes(last.reshape(3, 2, 3, 32), 1, 2)
    begin = spare[24:48].reshape(3, 8, 32)[:, :6]
    grad_first = jnp.transpose(begin.reshape(3, 2, 3, 32), (0, 2, 3, 1))
    return (
        grad_velocity,
        grad_first,
        spare[64],
        grad_hidden,
        jnp.stack([spare[56], spare[48]]),
        grad_last,
        spare[72, :2],
    )


def solution(mesh):
    cores = 2
    finer = Mesh(
        mesh.devices.reshape(mesh.shape["groups"], mesh.shape["gx"] // cores, cores), GROUPS_GX
    )
    placed = (P(None, GROUPS_GX, None), P(None, GROUPS_GX, None), P(), P(), P(), P(), P())
    return jax.shard_map(
        body,
        mesh=finer,
        in_specs=placed,
        out_specs=(
            P(None, GROUPS_GX, None),
            P("groups", None, None, None),
            P("groups"),
            P("groups", None, None, None, None),
            P("groups", None),
            P("groups", None, None, None),
            P("groups"),
        ),
        check_vma=False,
    )
```

time: 563 us -> 164 us (0.29); the launches traced: 556 us -> 164 us
  waiting for transfers between devices: 189 us -> 11.2 us
  starting transfers between devices: 146 us -> 39.1 us
  matrix products: 80.3 us -> 0 us
  blocking collectives: 12.6 us -> 73.4 us
  local copies, waits for them, and re-layouts: 53.3 us -> 12 us
  other arithmetic: 42.3 us -> 2.8 us
  between operations: 31.7 us -> 0.89 us
  Pallas kernels: 0 us -> 24.2 us
    all_to_all x10 -> x1, waiting for transfers between devices: 171 us -> 11.2 us  [body(): lax.all_to_all(sums.reshape(members, 1, 128), GX, 0, 0, tiled=True)]
    dot_general x33 -> x0, matrix products: 80.3 us -> none  [the longest x12 37.6 us: weight_terms(): jnp.einsum('oxy,qkxy->qok', error, stacked[:, :, p:p + count], precision=...]
    all_to_all x10 -> x1, starting transfers between devices: 94.9 us -> 15 us  [body(): lax.all_to_all(sums.reshape(members, 1, 128), GX, 0, 0, tiled=True)]
    ppermute x28 -> x0, starting transfers between devices: 46.3 us -> none  [the longest x14 35.8 us: padded_2(): lax.ppermute(head, axis, [((i + 1) % count, i) for i in range(count)])]
    all_to_all x1 -> x2, blocking collectives: 6.36 us -> 39.8 us  [the longest x1 34.1 us: total_of(): lax.all_to_all(half.reshape(far, -1, lanes), 'gx_0', 0, 0, tiled=True)]
    slice x78 -> x2, local copies, waits for them, and re-layouts: 28.4 us -> 0.59 us  [the longest x1 0.58 us: body(): spare[56]]
    all_to_all x1 -> x2, blocking collectives: 6.27 us -> 33.6 us  [from_everyone(): lax.all_to_all(jnp.broadcast_to(x[None], (length, *x.shape)), axis, 0, 0,...]
    pallas_call x0 -> x4, Pallas kernels: none -> 24.2 us  [the longest x1 12.7 us: body(): call(backward_kernel, (shape_of(2, rows, width), shape_of(192, 128)), [pl...]
  transfers between devices with their start and end apart: 40 -> 5, of which waited for: 23 -> 1; matrix products, arithmetic and copies ran while one was open for 23% -> 4% of each run, Pallas kernels for 0% -> 6%
where the time goes in v1:
time: 164 us
  blocking collectives  73.4 us (45%)
  starting transfers between devices  39.1 us (24%)
  Pallas kernels  24.2 us (15%)
  local copies, waits for them, and re-layouts  12 us (7%)
  waiting for transfers between devices  11.2 us (7%)
  other arithmetic  2.8 us (2%)
    all_to_all x1, blocking collectives, total_of(): lax.all_to_all(half.reshape(far, -1, lanes), 'gx_0', 0, 0, tiled=True)  34.1 us
    all_to_all x2, blocking collectives, from_everyone(): lax.all_to_all(jnp.broadcast_to(x[None], (length, *x.shape)), axis, 0, 0,...  33.6 us
    ppermute x4, starting transfers between devices, shifted(): return lax.ppermute(value, axis, pairs)  24 us
    all_to_all x1, starting transfers between devices, body(): lax.all_to_all(sums.reshape(members, 1, 128), GX, 0, 0, tiled=True)  15 us
    pallas_call x1, Pallas kernels, body(): call(backward_kernel, (shape_of(2, rows, width), shape_of(192, 128)), [pl...  12.7 us
    all_to_all x1, waiting for transfers between devices, body(): lax.all_to_all(sums.reshape(members, 1, 128), GX, 0, 0, tiled=True)  11.2 us
    pallas_call x1, Pallas kernels, body(): call(forward_kernel, tuple(held), [pltpu.VMEM((96 * BLOCK, 48), BF16), pl...  7.21 us
    all_to_all x1, blocking collectives, total_of(): lax.all_to_all(packed.reshape(near, lines // near, lanes), 'gx_1', 0, 0,...  5.74 us
  transfers between devices with their start and end apart: 5, of which 1 were waited for; matrix products, arithmetic and copies ran while one was open for 4% of the time, Pallas kernels for 6%

profile of v1, /device:TPU:37, one launch (start us, length us, event | category | flops | bytes accessed | tf_op | source)
XLA Modules:
  0.0 163.8 jit_solution(2066498386382269994)
XLA Ops:
  0.6 20.5 %collective-permute-start.7 = (f32[2,16,512]{2,1,0:T(8,128)}, f32[2,16,512]{2,1,0:T(8,128)S(1)}, u32[]{:S(2)}, u32[]{:S(2)}) collective-permute-start(f32[2,16,512]{2,1,0:T(8,128)} %vown.1), channel_id=1, source_target_pairs={{0,63},{1,0},{2,1},{3,2},{4,3},{5,4},{6,5},{7,6},{8,7},{9,8},{10,9... | collective-permute-start | bytes 196616 | tf_op jit(solution)/shard_map/ppermute | solution.py:31
  21.1 3.6 %collective-permute-start.5 = (f32[2,16,512]{2,1,0:T(8,128)}, f32[2,16,512]{2,1,0:T(8,128)S(1)}, u32[]{:S(2)}, u32[]{:S(2)}) collective-permute-start(f32[2,16,512]{2,1,0:T(8,128)} %cown.1), channel_id=1, source_target_pairs={{0,63},{1,0},{2,1},{3,2},{4,3},{5,4},{6,5},{7,6},{8,7},{9,8},{10,9... | collective-permute-start | bytes 196616 | tf_op jit(solution)/shard_map/ppermute | solution.py:31
  24.7 0.7 reverse_bitcast_fusion.3
  26.1 0.7 pad_maximum_fusion.4.out_taps
  26.9 1.0 slice_bitcast_fusion.6
  28.9 0.7 pad_maximum_fusion.3.wide
  30.5 2.3 %shard_map.126 = (f32[8,32,512]{2,1,0:T(8,128)}, f32[64,128]{1,0:T(8,128)}) custom-call(f32[2,16,512]{2,1,0:T(8,128)} %copy-done.3, f32[2,16,512]{2,1,0:T(8,128)S(1)} %copy-done, f32[2,16,512]{2,1,0:T(8,128)S(1)} %collective-permute-done.5.later.clater), custom_call_target="tpu_custom_call" | custom-call | tf_op jit(solution)/shard_map/pallas_call | solution.py:546
  32.8 15.0 %all-to-all-start.3 = ((f32[64,1,128]{2,1,0:T(1,128)}), f32[64,1,128]{2,1,0:T(1,128)S(1)}, u32[]{:S(2)}, u32[]{:S(2)}) async-start(f32[64,1,128]{2,1,0:T(1,128)} %bitcast.91), calls=%async_computation.3 | async-start | bytes 65536 | tf_op jit(solution)/shard_map/all_to_all | solution.py:549
  48.0 0.6 pad.32.narrow
  48.7 0.6 pad.36.narrow
  49.3 0.7 pad_maximum_fusion.2.wide
  50.0 0.7 copy-done.6
  50.7 0.7 broadcast_in_dim.28.bias
  51.4 7.2 %shard_map.128 = (bf16[832,512]{1,0:T(8,128)(2,1)}, bf16[832,512]{1,0:T(8,128)(2,1)}, bf16[768,512]{1,0:T(8,128)(2,1)}, bf16[768,512]{1,0:T(8,128)(2,1)}, bf16[7...) custom-call(f32[2,16,512]{2,1,0:T(8,128)} %copy-done.2, f32[2,16,512]{2,1,0:T(8,128)} %vown.1, f32[2,16,512]{2,1,0:T(8,128)} %copy-done.1, ...), custom_call_target="tpu_custom_call" | custom-call | tf_op jit(solution)/shard_map/pallas_call | solution.py:553
  58.7 11.2 %all-to-all-done.3 = f32[64,1,128]{2,1,0:T(1,128)S(1)} async-done(((f32[64,1,128]{2,1,0:T(1,128)}), f32[64,1,128]{2,1,0:T(1,128)S(1)}, u32[]{:S(2)}, u32[]{:S(2)}) %all-to-all-start.3) | async-done | bytes 32800 | tf_op jit(solution)/shard_map/all_to_all | solution.py:549
  69.8 0.6 copy-done.4
  70.5 2.0 %shard_map.127 = (f32[32,512]{1,0:T(8,128)S(1)}, s32[1,128]{1,0:T(1,128)}) custom-call(f32[64,128]{1,0:T(8,128)} %bitcast.84, f32[8,32,512]{2,1,0:T(8,128)} %get-tuple-element.57.basis), custom_call_target="tpu_custom_call" | custom-call | tf_op jit(solution)/shard_map/pallas_call | solution.py:563
  72.5 0.7 copy-done.8
  73.4 12.7 %shard_map.129 = (f32[2,16,512]{2,1,0:T(8,128)}, f32[192,128]{1,0:T(8,128)}) custom-call(f32[1,1]{1,0:T(1,128)} %constant.5.clone.1.factor, f32[32,512]{1,0:T(8,128)S(1)} %get-tuple-element.237.pressure, f32[2,16,512]{2,1,0:T(8,128)} %copy-done.3, f32[2,16,512]{2,1,0:T(8,128)S(1)} %copy-done, f32[2,16,512]{2,1,0:T(8,128)S(1)} %collective-permute-done.5.later.clater, ...), custom_call_target="tpu_custom_call" | custom-call | tf_op jit(solution)/shard_map/pallas_call | solution.py:577
  86.1 5.7 %all_to_all.43 = f32[2,96,128]{2,1,0:T(8,128)S(1)} all-to-all(f32[2,96,128]{2,1,0:T(8,128)} %bitcast.85), channel_id=1, replica_groups=mesh['groups'=4,'gx_0'=32,'gx_1'=2] {'gx_1'}, dimensions={0} | all-to-all | bytes 196608 | tf_op jit(solution)/shard_map/all_to_all | solution.py:485
  91.9 34.1 %all_to_all.44 = f32[32,3,128]{2,1,0:T(4,128)S(1)} all-to-all(f32[32,3,128]{2,1,0:T(4,128)S(1)} %reshape.94), channel_id=1, replica_groups=mesh['groups'=4,'gx_0'=32,'gx_1'=2] {'gx_0'}, dimensions={0} | all-to-all | bytes 98304 | tf_op jit(solution)/shard_map/all_to_all | solution.py:487
  126.0 26.6 %all_to_all.45 = f32[32,3,128]{2,1,0:T(4,128)S(1)} all-to-all(f32[32,3,128]{2,1,0:T(4,128)S(1)} %broadcast_in_dim.29), channel_id=1, replica_groups=mesh['groups'=4,'gx_0'=32,'gx_1'=2] {'gx_0'}, dimensions={0} | all-to-all | bytes 98304 | tf_op jit(solution)/shard_map/all_to_all | solution.py:25
  152.7 6.9 %all_to_all.46 = f32[2,96,128]{2,1,0:T(8,128)S(1)} all-to-all(f32[2,96,128]{2,1,0:T(8,128)S(1)} %broadcast_in_dim.31), channel_id=1, replica_groups=mesh['groups'=4,'gx_0'=32,'gx_1'=2] {'gx_1'}, dimensions={0} | all-to-all | bytes 196608 | tf_op jit(solution)/shard_map/all_to_all | solution.py:25
  162.4 0.7 copy.84
  (64 shorter events, 6.6 us)
Async XLA Ops:
  0.6 50.1 %collective-permute-start.7 = (f32[2,16,512]{2,1,0:T(8,128)}, f32[2,16,512]{2,1,0:T(8,128)S(1)}, u32[]{:S(2)}, u32[]{:S(2)}) collective-permute-start(f32[2,16,512]{2,1,0:T(8,128)} %vown.1), channel_id=1, source_target_pairs={{0,63},{1,0},{2,1},{3,2},{4,3},{5,4},{6,5},{7,6},{8,7},{9,8},{10,9... | collective-permute-start | bytes 196616 | tf_op jit(solution)/shard_map/ppermute | solution.py:31
  21.1 29.6 %collective-permute-start.6 = (f32[2,16,512]{2,1,0:T(8,128)}, f32[2,16,512]{2,1,0:T(8,128)S(1)}, u32[]{:S(2)}, u32[]{:S(2)}) collective-permute-start(f32[2,16,512]{2,1,0:T(8,128)} %vown.1), channel_id=1, source_target_pairs={{0,1},{1,2},{2,3},{3,4},{4,5},{5,6},{6,7},{7,8},{8,9},{9,10},{10,1... | collective-permute-start | bytes 196616 | tf_op jit(solution)/shard_map/ppermute | solution.py:31
  21.1 8.6 %collective-permute-start.5 = (f32[2,16,512]{2,1,0:T(8,128)}, f32[2,16,512]{2,1,0:T(8,128)S(1)}, u32[]{:S(2)}, u32[]{:S(2)}) collective-permute-start(f32[2,16,512]{2,1,0:T(8,128)} %cown.1), channel_id=1, source_target_pairs={{0,63},{1,0},{2,1},{3,2},{4,3},{5,4},{6,5},{7,6},{8,7},{9,8},{10,9... | collective-permute-start | bytes 196616 | tf_op jit(solution)/shard_map/ppermute | solution.py:31
  24.7 5.0 %collective-permute-start.4 = (f32[2,16,512]{2,1,0:T(8,128)}, f32[2,16,512]{2,1,0:T(8,128)S(1)}, u32[]{:S(2)}, u32[]{:S(2)}) collective-permute-start(f32[2,16,512]{2,1,0:T(8,128)} %cown.1), channel_id=1, source_target_pairs={{0,1},{1,2},{2,3},{3,4},{4,5},{5,6},{6,7},{7,8},{8,9},{9,10},{10,1... | collective-permute-start | bytes 196616 | tf_op jit(solution)/shard_map/ppermute | solution.py:31
  25.4 0.7 copy-start.5
  29.7 0.8 copy-start
  29.7 0.6 copy-start.3
  32.8 37.0 %all-to-all-start.3 = ((f32[64,1,128]{2,1,0:T(1,128)}), f32[64,1,128]{2,1,0:T(1,128)S(1)}, u32[]{:S(2)}, u32[]{:S(2)}) async-start(f32[64,1,128]{2,1,0:T(1,128)} %bitcast.91), calls=%async_computation.3 | async-start | bytes 65536 | tf_op jit(solution)/shard_map/all_to_all | solution.py:549
  50.0 0.7 copy-start.6
  50.0 0.7 copy-start.7
  50.7 0.7 copy-start.1
  50.7 0.7 copy-start.2
  69.8 0.6 copy-start.4
  72.5 0.7 copy-start.8

commit v2 on v1

--- a/solution.py
+++ b/solution.py
@@ -9,8 +9,9 @@
 from jax.sharding import PartitionSpec as P
 
 ITERS = 8
-GX = ("gx_0", "gx_1")
-GROUPS_GX = ("groups", "gx_0", "gx_1")
+FAR, NEAR, CORE = "gx_far", "gx_near", "gx_core"
+GX = (FAR, NEAR, CORE)
+GROUPS_GX = ("groups", FAR, NEAR, CORE)
 SPREAD_LIMIT = 3000.0
 BLOCK = 6
 SPAN = BLOCK + 2
@@ -479,14 +480,30 @@
     terms[96:192, :] = jnp.where(kept, middle0, 0.0) * scale
 
 
+def unpack_kernel(total, first, bias0, hidden, biases, last, ends):
+    for p in range(3):
+        for at, begin in enumerate((96, 0)):
+            block = total[begin : begin + 96, 32 * p : 32 * p + 32]
+            hidden[at, p] = block.reshape(3, 32, 32)
+    spare = turn(total[0:96, :], 32, 1)[:, :32]
+    for p in range(3):
+        for q in range(3):
+            for c in range(2):
+                at = 8 * p + 3 * c + q
+                last[p, q, c : c + 1] = spare[at : at + 1]
+                first[p, q, c : c + 1] = spare[24 + at : 25 + at]
+    biases[...] = jnp.concatenate([spare[56:57], spare[48:49]], axis=0)
+    bias0[...] = spare[64:65]
+    ends[...] = spare[72:73, :2]
+
+
 def total_of(packed):
-    far, near = lax.axis_size("gx_0"), lax.axis_size("gx_1")
     lines, lanes = packed.shape
-    half = lax.all_to_all(packed.reshape(near, lines // near, lanes), "gx_1", 0, 0, tiled=True)
-    half = half.sum(axis=0)
-    part = lax.all_to_all(half.reshape(far, -1, lanes), "gx_0", 0, 0, tiled=True).sum(axis=0)
-    half = from_everyone(part, "gx_0").reshape(lines // near, lanes)
-    return from_everyone(half, "gx_1").reshape(lines, lanes)
+    local = (NEAR, CORE)
+    part = packed.reshape(lax.axis_size(local), -1, lanes)
+    part = lax.all_to_all(part, local, 0, 0, tiled=True).sum(axis=0)
+    part = from_everyone(part, FAR).sum(axis=0)
+    return from_everyone(part, local).reshape(lines, lanes)
 
 
 def forward_taps(w):
@@ -518,12 +535,12 @@
     return jax.ShapeDtypeStruct(dims, dtype)
 
 
-def call(kernel, out_shape, scratch=(), **extra):
+def call(kernel, out_shape, scratch=(), room=63, **extra):
     return pl.pallas_call(
         kernel,
         out_shape=out_shape,
         scratch_shapes=list(scratch),
-        compiler_params=pltpu.CompilerParams(vmem_limit_bytes=60 * 1024 * 1024),
+        compiler_params=pltpu.CompilerParams(vmem_limit_bytes=room * 1024 * 1024),
         **extra,
     )
 
@@ -534,6 +551,14 @@
     cprev, clater = shifted(cotangent, GX, 1), shifted(cotangent, GX, -1)
     vprev, vlater = shifted(velocity, GX, 1), shifted(velocity, GX, -1)
 
+    basis, sums = call(
+        basis_kernel, (shape_of(ITERS, rows + 16, width), shape_of(members, 128))
+    )(cprev, cotangent, clater)
+    gathered = lax.all_to_all(sums.reshape(members, 1, 128), GX, 0, 0, tiled=True)
+
+    sums, w_first, b_first, w_hidden, b_hidden, w_last = lax.optimization_barrier(
+        (sums, w_first, b_first, w_hidden, b_hidden, w_last)
+    )
     wide_pad = ((0, 0), (0, 256 - 96))
     wide = jnp.stack([jnp.pad(forward_taps(w_hidden[m]), wide_pad) for m in range(2)])
     wide_back = jnp.stack([jnp.pad(backward_taps(w_hidden[m]), wide_pad) for m in range(2)])
@@ -542,11 +567,6 @@
     out_taps = out_taps_of(flipped(w_first))
     biases = jnp.stack([b_first, b_hidden[0], b_hidden[1]])
     biases = jnp.broadcast_to(biases[:, :, None], (3, biases.shape[1], 128))
-
-    basis, sums = call(
-        basis_kernel, (shape_of(ITERS, rows + 16, width), shape_of(members, 128))
-    )(cprev, cotangent, clater)
-    gathered = lax.all_to_all(sums.reshape(members, 1, 128), GX, 0, 0, tiled=True)
 
     heights = (rows + 10, rows + 8, rows + 6)
     held = [shape_of(h * 32, width, dtype=BF16) for h in heights for _ in range(2)]
@@ -586,6 +606,7 @@
             pltpu.VMEM((96 * BLOCK, 3 * SPAN * 32), BF16),
             pltpu.VMEM((96 * BLOCK, 48), BF16),
         ],
+        room=63,
         in_specs=[pl.BlockSpec(memory_space=pltpu.SMEM)] + [whole] * 16,
     )(
         factor.reshape(1, 1),
@@ -602,32 +623,33 @@
         out_taps,
     )
     total = total_of(terms)
-
-    def square(block):
-        return jnp.transpose(block.reshape(3, 32, 3, 32), (2, 0, 1, 3))
-
-    spare = total[:96, 96:]
-    grad_hidden = jnp.stack([square(total[96:, :96]), square(total[:96, :96])])
-    last = spare[:24].reshape(3, 8, 32)[:, :6]
-    grad_last = jnp.swapaxes(last.reshape(3, 2, 3, 32), 1, 2)
-    begin = spare[24:48].reshape(3, 8, 32)[:, :6]
-    grad_first = jnp.transpose(begin.reshape(3, 2, 3, 32), (0, 2, 3, 1))
+    taps = w_first.shape[0]
+    first, bias0, hidden, biases, last, ends = call(
+        unpack_kernel,
+        (
+            shape_of(taps, taps, 2, 32),
+            shape_of(1, 32),
+            shape_of(2, taps, taps, 32, 32),
+            shape_of(2, 32),
+            shape_of(taps, taps, 2, 32),
+            shape_of(1, 2),
+        ),
+    )(total)
     return (
         grad_velocity,
-        grad_first,
-        spare[64],
-        grad_hidden,
-        jnp.stack([spare[56], spare[48]]),
-        grad_last,
-        spare[72, :2],
+        jnp.swapaxes(first, 2, 3),
+        bias0.reshape(-1),
+        hidden,
+        biases,
+        last,
+        ends.reshape(-1),
     )
 
 
 def solution(mesh):
-    cores = 2
-    finer = Mesh(
-        mesh.devices.reshape(mesh.shape["groups"], mesh.shape["gx"] // cores, cores), GROUPS_GX
-    )
+    cores, near = 2, 4
+    far = mesh.shape["gx"] // (cores * near)
+    finer = Mesh(mesh.devices.reshape(mesh.shape["groups"], far, near, cores), GROUPS_GX)
     placed = (P(None, GROUPS_GX, None), P(None, GROUPS_GX, None), P(), P(), P(), P(), P())
     return jax.shard_map(
         body,

time: 164 us -> 143 us (0.87)
  blocking collectives: 73.4 us -> 59.3 us
  local copies, waits for them, and re-layouts: 12 us -> 7.47 us
  waiting for transfers between devices: 11.2 us -> 8.39 us
  Pallas kernels: 24.2 us -> 26 us
    all_to_all x2 -> x1, blocking collectives: 39.8 us -> 9.74 us  [total_of(): part = lax.all_to_all(part, local, 0, 0, tiled=True).sum(axis=0)]
    all_to_all x2, blocking collectives: 33.6 us -> 49.5 us  [from_everyone(): lax.all_to_all(jnp.broadcast_to(x[None], (length, *x.shape)), axis, 0, 0,...]
    all_to_all x1, waiting for transfers between devices: 11.2 us -> 7.44 us  [body(): lax.all_to_all(sums.reshape(members, 1, 128), GX, 0, 0, tiled=True)]
    unnamed x27 -> x24, local copies, waits for them, and re-layouts: 5.5 us -> 3.47 us
    pallas_call x0 -> x1, Pallas kernels: none -> 1.73 us  [body(): call(unpack_kernel, (shape_of(taps, taps, 2, 32), shape_of(1, 32), shape_...]
  transfers between devices with their start and end apart: 5 -> 5, of which waited for: 1 -> 2; matrix products, arithmetic and copies ran while one was open for 4% -> 4% of each run, Pallas kernels for 6% -> 7%
where the time goes in v2:
time: 143 us
  blocking collectives  59.3 us (41%)
  starting transfers between devices  38.6 us (27%)
  Pallas kernels  26 us (18%)
  waiting for transfers between devices  8.39 us (6%)
  local copies, waits for them, and re-layouts  7.47 us (5%)
  other arithmetic  2.09 us (1%)
    all_to_all x2, blocking collectives, from_everyone(): lax.all_to_all(jnp.broadcast_to(x[None], (length, *x.shape)), axis, 0, 0,...  49.5 us
    ppermute x4, starting transfers between devices, shifted(): return lax.ppermute(value, axis, pairs)  24 us
    all_to_all x1, starting transfers between devices, body(): lax.all_to_all(sums.reshape(members, 1, 128), GX, 0, 0, tiled=True)  14.6 us
    pallas_call x1, Pallas kernels, body(): call(backward_kernel, (shape_of(2, rows, width), shape_of(192, 128)), [pl...  12.7 us
    all_to_all x1, blocking collectives, total_of(): part = lax.all_to_all(part, local, 0, 0, tiled=True).sum(axis=0)  9.74 us
    all_to_all x1, waiting for transfers between devices, body(): lax.all_to_all(sums.reshape(members, 1, 128), GX, 0, 0, tiled=True)  7.44 us
    pallas_call x1, Pallas kernels, body(): call(forward_kernel, tuple(held), [pltpu.VMEM((96 * BLOCK, 48), BF16), pl...  7.19 us
    unnamed x24, local copies, waits for them, and re-layouts  3.47 us
  transfers between devices with their start and end apart: 5, of which 2 were waited for; matrix products, arithmetic and copies ran while one was open for 4% of the time, Pallas kernels for 7%

profile of v2, /device:TPU:37, one launch (start us, length us, event | category | flops | bytes accessed | tf_op | source)
XLA Modules:
  0.0 142.9 jit_solution(6926774756167468356)
XLA Ops:
  0.6 20.5 %collective-permute-start.5 = (f32[2,16,512]{2,1,0:T(8,128)}, f32[2,16,512]{2,1,0:T(8,128)S(1)}, u32[]{:S(2)}, u32[]{:S(2)}) collective-permute-start(f32[2,16,512]{2,1,0:T(8,128)} %cown.1), channel_id=1, source_target_pairs={{0,63},{1,0},{2,1},{3,2},{4,3},{5,4},{6,5},{7,6},{8,7},{9,8},{10,9... | collective-permute-start | bytes 196616 | tf_op jit(solution)/shard_map/ppermute | solution.py:32
  21.1 3.6 %collective-permute-start.7 = (f32[2,16,512]{2,1,0:T(8,128)}, f32[2,16,512]{2,1,0:T(8,128)S(1)}, u32[]{:S(2)}, u32[]{:S(2)}) collective-permute-start(f32[2,16,512]{2,1,0:T(8,128)} %vown.1), channel_id=1, source_target_pairs={{0,63},{1,0},{2,1},{3,2},{4,3},{5,4},{6,5},{7,6},{8,7},{9,8},{10,9... | collective-permute-start | bytes 196616 | tf_op jit(solution)/shard_map/ppermute | solution.py:32
  24.7 0.9 collective-permute-done.4.prev.cprev
  25.6 0.6 copy-done.2
  26.2 2.4 %shard_map.126 = (f32[8,32,512]{2,1,0:T(8,128)}, f32[64,128]{1,0:T(8,128)}) custom-call(f32[2,16,512]{2,1,0:T(8,128)} %copy-done.2, f32[2,16,512]{2,1,0:T(8,128)} %cown.1, f32[2,16,512]{2,1,0:T(8,128)S(1)} %collective-permute-done.5.later.clater), custom_call_target="tpu_custom_call" | custom-call | tf_op jit(solution)/shard_map/pallas_call | solution.py:554
  28.6 14.6 %all-to-all-start.3 = ((f32[64,1,128]{2,1,0:T(1,128)}), f32[64,1,128]{2,1,0:T(1,128)S(1)}, u32[]{:S(2)}, u32[]{:S(2)}) async-start(f32[64,1,128]{2,1,0:T(1,128)} %bitcast.63), calls=%async_computation.3 | async-start | bytes 65536 | tf_op jit(solution)/shard_map/all_to_all | solution.py:557
  43.2 0.7 reverse_bitcast_fusion.3
  44.0 0.7 copy-done.6
  44.7 0.7 pad_maximum_fusion.3.out_taps
  46.4 0.7 pad_maximum_fusion.1.wide
  47.1 0.7 copy-done.7
  47.9 0.6 pad.32.narrow
  48.6 0.6 pad.36.narrow
  49.5 0.7 broadcast_in_dim.15.bias
  50.2 7.2 %shard_map.128 = (bf16[832,512]{1,0:T(8,128)(2,1)}, bf16[832,512]{1,0:T(8,128)(2,1)}, bf16[768,512]{1,0:T(8,128)(2,1)}, bf16[768,512]{1,0:T(8,128)(2,1)}, bf16[7...) custom-call(f32[2,16,512]{2,1,0:T(8,128)} %copy-done.4, f32[2,16,512]{2,1,0:T(8,128)} %vown.1, f32[2,16,512]{2,1,0:T(8,128)} %copy-done.3, ...), custom_call_target="tpu_custom_call" | custom-call | tf_op jit(solution)/shard_map/pallas_call | solution.py:573
  57.4 0.7 pad_maximum_fusion.2.wide
  58.1 7.4 %all-to-all-done.3 = f32[64,1,128]{2,1,0:T(1,128)S(1)} async-done(((f32[64,1,128]{2,1,0:T(1,128)}), f32[64,1,128]{2,1,0:T(1,128)S(1)}, u32[]{:S(2)}, u32[]{:S(2)}) %all-to-all-start.3) | async-done | bytes 32800 | tf_op jit(solution)/shard_map/all_to_all | solution.py:557
  66.2 2.0 %shard_map.127 = (f32[32,512]{1,0:T(8,128)S(1)}, s32[1,128]{1,0:T(1,128)}) custom-call(f32[64,128]{1,0:T(8,128)} %bitcast.60, f32[8,32,512]{2,1,0:T(8,128)} %get-tuple-element.68.basis), custom_call_target="tpu_custom_call" | custom-call | tf_op jit(solution)/shard_map/pallas_call | solution.py:583
  68.2 0.7 copy-done.9
  69.2 12.7 %shard_map.129 = (f32[2,16,512]{2,1,0:T(8,128)}, f32[192,128]{1,0:T(8,128)}) custom-call(f32[1,1]{1,0:T(1,128)} %constant.5.clone.1.factor, f32[32,512]{1,0:T(8,128)S(1)} %get-tuple-element.224.pressure, f32[2,16,512]{2,1,0:T(8,128)} %copy-done.2, f32[2,16,512]{2,1,0:T(8,128)S(1)} %copy-done, f32[2,16,512]{2,1,0:T(8,128)S(1)} %collective-permute-done.5.later.clater, ...), custom_call_target="tpu_custom_call" | custom-call | tf_op jit(solution)/shard_map/pallas_call | solution.py:597
  81.8 9.7 %all_to_all.38 = f32[8,24,128]{2,1,0:T(8,128)S(1)} all-to-all(f32[8,24,128]{2,1,0:T(8,128)} %bitcast.61), channel_id=1, replica_groups=mesh['groups'=4,'gx_far'=8,'gx_near'=4,'gx_core'=2] {'gx_near','gx_core'}, dimensions={0} | all-to-all | bytes 196608 | tf_op jit(solution)/shard_map/all_to_all | solution.py:504
  91.6 36.2 %all_to_all.39 = f32[8,24,128]{2,1,0:T(8,128)S(1)} all-to-all(f32[8,24,128]{2,1,0:T(8,128)S(1)} %broadcast_in_dim.16), channel_id=1, replica_groups=mesh['groups'=4,'gx_far'=8,'gx_near'=4,'gx_core'=2] {'gx_far'}, dimensions={0} | all-to-all | bytes 196608 | tf_op jit(solution)/shard_map/all_to_all | solution.py:26
  127.9 13.3 %all_to_all.40 = f32[8,24,128]{2,1,0:T(8,128)} all-to-all(f32[8,24,128]{2,1,0:T(8,128)S(1)} %broadcast_in_dim.17), channel_id=1, replica_groups=mesh['groups'=4,'gx_far'=8,'gx_near'=4,'gx_core'=2] {'gx_near','gx_core'}, dimensions={0} | all-to-all | bytes 196608 | tf_op jit(solution)/shard_map/all_to_all | solution.py:26
  141.2 1.7 %shard_map.130 = (f32[3,3,2,32]{3,2,1,0:T(2,128)}, f32[1,32]{1,0:T(1,128)}, f32[2,3,3,32,32]{4,3,2,1,0:T(8,128)}, f32[2,32]{1,0:T(2,128)}, f32[3,3,2,32]{3,2,1,0:T(2,128)}, /*index=5*/f32[1,2]{1,0:T(1,128)}) custom-call(f32[192,128]{1,0:T(8,128)} %bitcast.59), custom_call_target="tpu_custom_call" | custom-call | tf_op jit(solution)/shard_map/pallas_call | solution.py:627
  (51 shorter events, 2.4 us)
Async XLA Ops:
  0.6 44.9 %copy-start.1 = (f32[2,3,3,32,32]{4,3,2,1,0:T(8,128)S(1)}, f32[2,3,3,32,32]{4,3,2,1,0:T(8,128)}, u32[]{:S(2)}) copy-start(f32[2,3,3,32,32]{4,3,2,1,0:T(8,128)} %param.15) | copy-start | bytes 221188
  0.6 24.0 %collective-permute-start.5 = (f32[2,16,512]{2,1,0:T(8,128)}, f32[2,16,512]{2,1,0:T(8,128)S(1)}, u32[]{:S(2)}, u32[]{:S(2)}) collective-permute-start(f32[2,16,512]{2,1,0:T(8,128)} %cown.1), channel_id=1, source_target_pairs={{0,63},{1,0},{2,1},{3,2},{4,3},{5,4},{6,5},{7,6},{8,7},{9,8},{10,9... | collective-permute-start | bytes 196616 | tf_op jit(solution)/shard_map/ppermute | solution.py:32
  21.1 4.5 %collective-permute-start.4 = (f32[2,16,512]{2,1,0:T(8,128)}, f32[2,16,512]{2,1,0:T(8,128)S(1)}, u32[]{:S(2)}, u32[]{:S(2)}) collective-permute-start(f32[2,16,512]{2,1,0:T(8,128)} %cown.1), channel_id=1, source_target_pairs={{0,1},{1,2},{2,3},{3,4},{4,5},{5,6},{6,7},{7,8},{8,9},{9,10},{10,1... | collective-permute-start | bytes 196616 | tf_op jit(solution)/shard_map/ppermute | solution.py:32
  21.1 28.4 %collective-permute-start.7 = (f32[2,16,512]{2,1,0:T(8,128)}, f32[2,16,512]{2,1,0:T(8,128)S(1)}, u32[]{:S(2)}, u32[]{:S(2)}) collective-permute-start(f32[2,16,512]{2,1,0:T(8,128)} %vown.1), channel_id=1, source_target_pairs={{0,63},{1,0},{2,1},{3,2},{4,3},{5,4},{6,5},{7,6},{8,7},{9,8},{10,9... | collective-permute-start | bytes 196616 | tf_op jit(solution)/shard_map/ppermute | solution.py:32
  24.7 24.8 %collective-permute-start.6 = (f32[2,16,512]{2,1,0:T(8,128)}, f32[2,16,512]{2,1,0:T(8,128)S(1)}, u32[]{:S(2)}, u32[]{:S(2)}) collective-permute-start(f32[2,16,512]{2,1,0:T(8,128)} %vown.1), channel_id=1, source_target_pairs={{0,1},{1,2},{2,3},{3,4},{4,5},{5,6},{6,7},{7,8},{8,9},{9,10},{10,1... | collective-permute-start | bytes 196616 | tf_op jit(solution)/shard_map/ppermute | solution.py:32
  25.6 0.6 copy-start.2
  28.6 36.9 %all-to-all-start.3 = ((f32[64,1,128]{2,1,0:T(1,128)}), f32[64,1,128]{2,1,0:T(1,128)S(1)}, u32[]{:S(2)}, u32[]{:S(2)}) async-start(f32[64,1,128]{2,1,0:T(1,128)} %bitcast.63), calls=%async_computation.3 | async-start | bytes 65536 | tf_op jit(solution)/shard_map/all_to_all | solution.py:557
  44.0 0.7 copy-start.6
  47.1 0.7 copy-start.7
  47.1 0.7 copy-start.8
  49.5 0.7 copy-start.3
  49.5 0.7 copy-start.4
  65.6 0.6 copy-start.5
  66.2 2.8 %copy-start = (f32[2,16,512]{2,1,0:T(8,128)S(1)}, f32[2,16,512]{2,1,0:T(8,128)}, u32[]{:S(2)}) copy-start(f32[2,16,512]{2,1,0:T(8,128)} %cown.1) | copy-start | bytes 196612
  68.2 0.7 copy-start.9

commit v3 on v2

--- a/solution.py
+++ b/solution.py
@@ -1,5 +1,3 @@
-import functools
-
 import jax
 import jax.numpy as jnp
 from jax import lax
@@ -7,6 +5,7 @@
 from jax.experimental.pallas import tpu as pltpu
 from jax.sharding import Mesh
 from jax.sharding import PartitionSpec as P
+
 
 ITERS = 8
 FAR, NEAR, CORE = "gx_far", "gx_near", "gx_core"
@@ -62,11 +61,13 @@
     return turn(t, 1, 0) + turn(t, -1, 0) + turn(t, 1, 1) + turn(t, -1, 1)
 
 
-def basis_kernel(prev, own, later, basis, sums):
+def basis_kernel(prev, own, later, basis, sums, around):
     rows = own.shape[1]
     first = jnp.concatenate([prev[0], own[0], later[0]], axis=0)
     second = jnp.concatenate([prev[1], own[1], later[1]], axis=0)
     source = -(turn(first, -1, 0) - first + (turn(second, -1, 1) - second))
+    around[0] = first[rows - 8 : 2 * rows + 8]
+    around[1] = second[rows - 8 : 2 * rows + 8]
     line = lax.broadcasted_iota(jnp.int32, (2 * ITERS, 128), 0)
     lane = lax.broadcasted_iota(jnp.int32, (2 * ITERS, 128), 1)
     squares, crosses = [], []
@@ -168,7 +169,7 @@
         term = jnp.concatenate([answer[k]] * wide, axis=1) * basis[k]
         lam = term if lam is None else lam + term
     pressure[...] = lam
-    unsafe[...] = jnp.where(safe, 0, 1).astype(jnp.int32)
+    unsafe[0, 0] = jnp.max(jnp.where(safe, 0.0, 1.0)).astype(jnp.int32)
 
 
 def laplace(field):
@@ -184,9 +185,9 @@
     return jnp.sum(from_everyone(local, GX)[:, 0, 0])
 
 
-def stepwise_pressure(cotangent, later):
-    first, second = cotangent[0], cotangent[1]
-    below = jnp.concatenate([first[1:], later[0, :1]], axis=0)
+def stepwise_pressure(around):
+    first, second = around[0, 8:-8], around[1, 8:-8]
+    below = around[0, 9:-7]
     source = -(below - first + (jnp.roll(second, -1, 1) - second))
 
     def iterate(_, carry):
@@ -265,7 +266,28 @@
 
 
 def forward_kernel(
-    prev, own, later, narrow, wide, bias, a0h, a0l, a1h, a1l, a2h, a2l, weights0, weights1, weights2
+    prev,
+    own,
+    later,
+    narrow,
+    wide,
+    bias,
+    narrow_back,
+    wide_back,
+    out_taps,
+    a0h,
+    a0l,
+    a1h,
+    a1l,
+    a2h,
+    a2l,
+    band2,
+    band1,
+    band0,
+    band_out,
+    weights0,
+    weights1,
+    weights2,
 ):
     rows, width = own.shape[1], own.shape[2]
     v = [jnp.concatenate([prev[c, rows - 8 :], own[c], later[c, :8]], axis=0) for c in range(2)]
@@ -282,6 +304,12 @@
     for s in starts(-3, rows + 6):
         x = take((a1h, a1l), s + 3, SPAN)
         put((a2h, a2l), s + 3, jnp.tanh(wide_conv(weights2[...], *x) + shift[2]))
+    band2[...] = banded_narrow(narrow_back[...])
+    band1[...] = banded(wide_back[1])
+    band0[...] = banded(wide_back[0])
+    high, low = banded_out(out_taps[...], rows)
+    band_out[0] = high
+    band_out[1] = low
 
 
 def dot_nt(a, b):
@@ -327,27 +355,26 @@
     column = jnp.sum(fold_lanes(jnp.sum(e, axis=0)), axis=1, keepdims=True)
     line = lax.broadcasted_iota(jnp.int32, (32, 128), 0)
     lane = lax.broadcasted_iota(jnp.int32, (32, 128), 1)
-    return eight_rows(jnp.sum(jnp.where(lane == line + 96, column, 0.0), axis=0, keepdims=True))
+    return jnp.sum(jnp.where(lane == line + 96, column, 0.0), axis=0, keepdims=True)
 
 
 def backward_kernel(
     factor,
     pressure,
-    cprev,
-    cown,
-    clater,
+    around,
     vprev,
     vown,
     vlater,
-    a0h,
-    a0l,
-    a1h,
-    a1l,
-    a2h,
-    a2l,
-    narrow,
-    wide,
-    out_taps,
+    far2,
+    far2h,
+    far2l,
+    far1,
+    far1h,
+    far1l,
+    far0,
+    far0h,
+    far0l,
+    far_out,
     grad_velocity,
     terms,
     e2,
@@ -355,21 +382,32 @@
     e0,
     eh,
     el,
-    weights,
-    weights_narrow,
+    band2,
+    a2h,
+    a2l,
+    band1,
+    a1h,
+    a1l,
+    band0,
+    a0h,
+    a0l,
+    band_out,
+    arrived,
 ):
     rows, width = vown.shape[1], vown.shape[2]
     a0, a1, a2, split = (a0h, a0l), (a1h, a1l), (a2h, a2l), (eh, el)
-
-    def extended(prev, own, later, c):
-        return jnp.concatenate([prev[c, rows - 8 :], own[c], later[c, :8]], axis=0)
+    sources = (far2, far2h, far2l, far1, far1h, far1l, far0, far0h, far0l, far_out)
+    targets = (band2, a2h, a2l, band1, a1h, a1l, band0, a0h, a0l, band_out)
+    copies = [
+        pltpu.make_async_copy(source, target, arrived.at[i])
+        for i, (source, target) in enumerate(zip(sources, targets))
+    ]
+    for copy in copies:
+        copy.start()
 
     lam = pressure[...]
-    adjoint = [
-        extended(cprev, cown, clater, 0) - (lam - turn(lam, 1, 0)),
-        extended(cprev, cown, clater, 1) - (lam - turn(lam, 1, 1)),
-    ]
-    v = [extended(vprev, vown, vlater, c) for c in range(2)]
+    adjoint = [around[0] - (lam - turn(lam, 1, 0)), around[1] - (lam - turn(lam, 1, 1))]
+    v = [jnp.concatenate([vprev[c, rows - 8 :], vown[c], vlater[c, :8]], axis=0) for c in range(2)]
     e3 = [step_size * item for item in adjoint]
 
     def slope_of(act, at):
@@ -381,32 +419,34 @@
         put(split, at, value)
         ref[pl.ds(at * 32, BLOCK * 32), :] = value.reshape(BLOCK * 32, width)
 
-    weights_narrow[...] = banded_narrow(narrow[...])
+    for copy in copies[:3]:
+        copy.wait()
     for s in starts(-3, rows + 6):
         pair = [e3[c][s + 7 : s + 7 + SPAN] for c in range(2)]
-        keep(e2, s + 3, narrow_conv(weights_narrow[...], pair) * slope_of(a2, s + 3))
-    weights[...] = banded(wide[1])
+        keep(e2, s + 3, narrow_conv(band2[...], pair) * slope_of(a2, s + 3))
+    for copy in copies[3:6]:
+        copy.wait()
     for s in starts(-2, rows + 4):
         x = take(split, s + 2, SPAN)
         e1[pl.ds((s + 2) * 32, BLOCK * 32), :] = (
-            wide_conv(weights[...], *x) * slope_of(a1, s + 4)
+            wide_conv(band1[...], *x) * slope_of(a1, s + 4)
         ).reshape(BLOCK * 32, width)
     split_rows = (rows + 4) * 32
     high, low = halves(e1[...])
     eh[0:split_rows, :] = high
     el[0:split_rows, :] = low
-    weights[...] = banded(wide[0])
+    for copy in copies[6:]:
+        copy.wait()
     for s in starts(-1, rows + 2):
         x = take(split, s + 1, SPAN)
         e0[pl.ds((s + 1) * 32, BLOCK * 32), :] = (
-            wide_conv(weights[...], *x) * slope_of(a0, s + 5)
+            wide_conv(band0[...], *x) * slope_of(a0, s + 5)
         ).reshape(BLOCK * 32, width)
 
     own = slice(8, 8 + rows)
-    wh, wl = banded_out(out_taps, rows)
     high, low = halves(e0[...])
     cells = (rows + 2) * 32
-    wh, wl = wh[:, :cells], wl[:, :cells]
+    wh, wl = band_out[0, :, :cells], band_out[1, :, :cells]
     y = (
         jnp.dot(wh, high, preferred_element_type=F32)
         + jnp.dot(wh, low, preferred_element_type=F32)
@@ -445,10 +485,14 @@
     last = last.reshape(6, rows, (rows + 4) * 32)
     group = lax.broadcasted_iota(jnp.int32, (rows, (rows + 4) * 32), 1) // 32
     line = lax.broadcasted_iota(jnp.int32, (rows, (rows + 4) * 32), 0)
-    spare = []
-    for p in range(3):
-        picked = jnp.sum(jnp.where((group == line + p)[None], last, 0.0), axis=1)
-        spare.append(eight_rows(lane_groups_summed(picked)))
+    last = [
+        eight_rows(
+            lane_groups_summed(
+                jnp.sum(jnp.where((group == line + p)[None], last, 0.0), axis=1)
+            )
+        )
+        for p in range(3)
+    ]
 
     inner = jnp.concatenate(
         [jnp.concatenate([turn(f, 1, 1), f, turn(f, -1, 1)], axis=0) for f in v], axis=0
@@ -460,41 +504,58 @@
     begin = begin.reshape(6, tall, rows * 32)
     group = lax.broadcasted_iota(jnp.int32, (tall, rows * 32), 1) // 32
     line = lax.broadcasted_iota(jnp.int32, (tall, rows * 32), 0)
-    for p in range(3):
-        picked = jnp.sum(jnp.where((line == group + p + 7)[None], begin, 0.0), axis=1)
-        spare.append(eight_rows(lane_groups_summed(picked)))
-
-    spare.append(bias_line(e2, 3, rows))
-    spare.append(bias_line(e1, 2, rows))
-    spare.append(bias_line(e0, 1, rows))
+    begin = [
+        eight_rows(
+            lane_groups_summed(
+                jnp.sum(jnp.where((line == group + p + 7)[None], begin, 0.0), axis=1)
+            )
+        )
+        for p in range(3)
+    ]
+
     lane = lax.broadcasted_iota(jnp.int32, (1, 128), 1)
     ends = jnp.zeros((1, 128), F32)
     for c in range(2):
         end = jnp.sum(jnp.sum(e3[c][own], axis=0, keepdims=True), axis=1, keepdims=True)
         ends = ends + jnp.where(lane == 96 + c, end, 0.0)
-    spare.append(eight_rows(ends))
-    spare.append(jnp.zeros((96 - 8 * len(spare), 128), F32))
-    spare = jnp.concatenate(spare, axis=0)
-    kept = lax.broadcasted_iota(jnp.int32, (96, 128), 1) < 96
-    terms[0:96, :] = jnp.where(kept, middle1, spare) * scale
-    terms[96:192, :] = jnp.where(kept, middle0, 0.0) * scale
+    sums = [bias_line(e2, 3, rows), bias_line(e1, 2, rows), bias_line(e0, 1, rows), ends]
+    sums = eight_rows(jnp.concatenate(sums, axis=0))
+    place = lax.broadcasted_iota(jnp.int32, (8, 128), 1) // 32
+
+    def merged(parts, rest):
+        for p, part in enumerate(parts):
+            rest = jnp.where(place == p, part, rest)
+        return rest
+
+    terms[0:72, :] = dense(middle1) * scale
+    terms[72:144, :] = dense(middle0) * scale
+    terms[144:152, :] = merged(last, sums) * scale
+    terms[152:160, :] = merged(begin, jnp.zeros_like(sums)) * scale
+
+
+def dense(x):
+    flat = jnp.concatenate([x[:, 32 * p : 32 * p + 32] for p in range(3)], axis=0)
+    return jnp.concatenate([flat[72 * g : 72 * g + 72] for g in range(4)], axis=1)
+
+
+def sparse(x):
+    flat = jnp.concatenate([x[:, 32 * g : 32 * g + 32] for g in range(4)], axis=0)
+    return [flat[96 * p : 96 * p + 96] for p in range(3)]
 
 
 def unpack_kernel(total, first, bias0, hidden, biases, last, ends):
+    for at, begin in enumerate((72, 0)):
+        for p, block in enumerate(sparse(total[begin : begin + 72, :])):
+            hidden[at, p] = block.reshape(3, 32, 32)
     for p in range(3):
-        for at, begin in enumerate((96, 0)):
-            block = total[begin : begin + 96, 32 * p : 32 * p + 32]
-            hidden[at, p] = block.reshape(3, 32, 32)
-    spare = turn(total[0:96, :], 32, 1)[:, :32]
-    for p in range(3):
-        for q in range(3):
-            for c in range(2):
-                at = 8 * p + 3 * c + q
-                last[p, q, c : c + 1] = spare[at : at + 1]
-                first[p, q, c : c + 1] = spare[24 + at : 25 + at]
-    biases[...] = jnp.concatenate([spare[56:57], spare[48:49]], axis=0)
-    bias0[...] = spare[64:65]
-    ends[...] = spare[72:73, :2]
+        for ref, begin in ((last, 144), (first, 152)):
+            part = total[begin : begin + 8, 32 * p : 32 * p + 32]
+            for q in range(3):
+                ref[p, q] = jnp.concatenate([part[q : q + 1], part[3 + q : 4 + q]], axis=0)
+    sums = total[144:152, 96:128]
+    biases[...] = jnp.concatenate([sums[1:2], sums[0:1]], axis=0)
+    bias0[...] = sums[2:3]
+    ends[...] = sums[3:4, :2]
 
 
 def total_of(packed):
@@ -549,16 +610,22 @@
     rows, width = velocity.shape[1], velocity.shape[2]
     members = lax.axis_size(GX)
     cprev, clater = shifted(cotangent, GX, 1), shifted(cotangent, GX, -1)
-    vprev, vlater = shifted(velocity, GX, 1), shifted(velocity, GX, -1)
-
-    basis, sums = call(
-        basis_kernel, (shape_of(ITERS, rows + 16, width), shape_of(members, 128))
+    basis, sums, around = call(
+        basis_kernel,
+        (
+            shape_of(ITERS, rows + 16, width),
+            shape_of(members, 128),
+            shape_of(2, rows + 16, width),
+        ),
+        room=16,
     )(cprev, cotangent, clater)
     gathered = lax.all_to_all(sums.reshape(members, 1, 128), GX, 0, 0, tiled=True)
 
     sums, w_first, b_first, w_hidden, b_hidden, w_last = lax.optimization_barrier(
         (sums, w_first, b_first, w_hidden, b_hidden, w_last)
     )
+    sums, velocity = lax.optimization_barrier((sums, velocity))
+    vprev, vlater = shifted(velocity, GX, 1), shifted(velocity, GX, -1)
     wide_pad = ((0, 0), (0, 256 - 96))
     wide = jnp.stack([jnp.pad(forward_taps(w_hidden[m]), wide_pad) for m in range(2)])
     wide_back = jnp.stack([jnp.pad(backward_taps(w_hidden[m]), wide_pad) for m in range(2)])
@@ -570,58 +637,51 @@
 
     heights = (rows + 10, rows + 8, rows + 6)
     held = [shape_of(h * 32, width, dtype=BF16) for h in heights for _ in range(2)]
-    actives = call(
+    wide_band = shape_of(96 * BLOCK, 3 * SPAN * 32, dtype=BF16)
+    narrow_band = shape_of(96 * BLOCK, 48, dtype=BF16)
+    edge = -(-(rows + 2) * 32 // 128) * 128
+    held += [narrow_band, wide_band, wide_band, shape_of(2, 6 * rows, edge, dtype=BF16)]
+    a0h, a0l, a1h, a1l, a2h, a2l, band2, band1, band0, band_out = call(
         forward_kernel,
         tuple(held),
-        [
-            pltpu.VMEM((96 * BLOCK, 48), BF16),
-            pltpu.VMEM((96 * BLOCK, 3 * SPAN * 32), BF16),
-            pltpu.VMEM((96 * BLOCK, 3 * SPAN * 32), BF16),
-        ],
-    )(vprev, velocity, vlater, narrow, wide, biases)
+        [pltpu.VMEM(item.shape, item.dtype) for item in (narrow_band, wide_band, wide_band)],
+    )(vprev, velocity, vlater, narrow, wide, biases, narrow_back, wide_back, out_taps)
 
     quick, unsafe = call(
-        pressure_kernel, (shape_of(rows + 16, width), shape_of(1, 128, dtype=jnp.int32))
+        pressure_kernel,
+        (shape_of(rows + 16, width), shape_of(1, 1, dtype=jnp.int32)),
+        room=12,
+        out_specs=(
+            pl.BlockSpec(memory_space=pltpu.VMEM),
+            pl.BlockSpec(memory_space=pltpu.SMEM),
+        ),
     )(gathered.reshape(members, 128), basis)
     pressure = lax.cond(
         unsafe[0, 0] != 0,
-        lambda c, l, _: stepwise_pressure(c, l),
-        lambda c, l, q: q,
-        cotangent,
-        clater,
+        lambda c, _: stepwise_pressure(c),
+        lambda c, q: q,
+        around,
         quick,
     )
 
     factor = 1.0 / jnp.sqrt(jnp.float32(members * rows * width))
     whole = pl.BlockSpec(memory_space=pltpu.VMEM)
+    outside = pl.BlockSpec(memory_space=pl.ANY)
+    fetched = (band2, a2h, a2l, band1, a1h, a1l, band0, a0h, a0l, band_out)
     grad_velocity, terms = call(
         backward_kernel,
-        (shape_of(2, rows, width), shape_of(192, 128)),
+        (shape_of(2, rows, width), shape_of(160, 128)),
         [
             pltpu.VMEM(((rows + 6) * 32, width), F32),
             pltpu.VMEM(((rows + 4) * 32, width), F32),
             pltpu.VMEM(((rows + 2) * 32, width), F32),
             pltpu.VMEM(((rows + 6) * 32, width), BF16),
             pltpu.VMEM(((rows + 6) * 32, width), BF16),
-            pltpu.VMEM((96 * BLOCK, 3 * SPAN * 32), BF16),
-            pltpu.VMEM((96 * BLOCK, 48), BF16),
-        ],
-        room=63,
-        in_specs=[pl.BlockSpec(memory_space=pltpu.SMEM)] + [whole] * 16,
-    )(
-        factor.reshape(1, 1),
-        pressure,
-        cprev,
-        cotangent,
-        clater,
-        vprev,
-        velocity,
-        vlater,
-        *actives,
-        narrow_back,
-        wide_back,
-        out_taps,
-    )
+        ]
+        + [pltpu.VMEM(item.shape, item.dtype) for item in fetched]
+        + [pltpu.SemaphoreType.DMA((len(fetched),))],
+        in_specs=[pl.BlockSpec(memory_space=pltpu.SMEM)] + [whole] * 5 + [outside] * len(fetched),
+    )(factor.reshape(1, 1), pressure, around, vprev, velocity, vlater, *fetched)
     total = total_of(terms)
     taps = w_first.shape[0]
     first, bias0, hidden, biases, last, ends = call(

time: 143 us -> 143 us (level)
  waiting for transfers between devices: 8.39 us -> 6.28 us
    reshape x0 -> x2, local copies, waits for them, and re-layouts: none -> 1.55 us  [the longest x1 0.89 us: total_of(): part = packed.reshape(lax.axis_size(local), -1, lanes)]
    unnamed x24 -> x18, local copies, waits for them, and re-layouts: 3.47 us -> 2.4 us
  transfers between devices with their start and end apart: 5 -> 5, of which waited for: 2 -> 1; matrix products, arithmetic and copies ran while one was open for 4% -> 4% of each run, Pallas kernels for 7% -> 7%
where the time goes in v3:
time: 143 us; the launch traced here: 142 us
  blocking collectives  59.4 us (42%)
  starting transfers between devices  39.8 us (28%)
  Pallas kernels  24.8 us (17%)
  local copies, waits for them, and re-layouts  7.94 us (6%)
  waiting for transfers between devices  6.28 us (4%)
  other arithmetic  2.09 us (1%)
  between operations  1.46 us (1%)
    all_to_all x2, blocking collectives, from_everyone(): lax.all_to_all(jnp.broadcast_to(x[None], (length, *x.shape)), axis, 0, 0,...  50.1 us
    ppermute x4, starting transfers between devices, shifted(): return lax.ppermute(value, axis, pairs)  24.1 us
    all_to_all x1, starting transfers between devices, body(): lax.all_to_all(sums.reshape(members, 1, 128), GX, 0, 0, tiled=True)  15.7 us
    pallas_call x1, Pallas kernels, body(): call(backward_kernel, (shape_of(2, rows, width), shape_of(160, 128)), [pl...  12.7 us
    all_to_all x1, blocking collectives, total_of(): part = lax.all_to_all(part, local, 0, 0, tiled=True).sum(axis=0)  9.3 us
    pallas_call x1, Pallas kernels, body(): call(forward_kernel, tuple(held), [pltpu.VMEM(item.shape, item.dtype) for...  7.88 us
    all_to_all x1, waiting for transfers between devices, body(): lax.all_to_all(sums.reshape(members, 1, 128), GX, 0, 0, tiled=True)  6.27 us
  transfers between devices with their start and end apart: 5, of which 1 were waited for; matrix products, arithmetic and copies ran while one was open for 4% of the time, Pallas kernels for 7%

profile of v3, /device:TPU:37, one launch (start us, length us, event | category | flops | bytes accessed | tf_op | source)
XLA Modules:
  0.0 141.9 jit_solution(6384036658869750791)
XLA Ops:
  0.6 3.2 %collective-permute-start.4 = (f32[2,16,512]{2,1,0:T(8,128)}, f32[2,16,512]{2,1,0:T(8,128)S(1)}, u32[]{:S(2)}, u32[]{:S(2)}) collective-permute-start(f32[2,16,512]{2,1,0:T(8,128)} %own.1), channel_id=1, source_target_pairs={{0,1},{1,2},{2,3},{3,4},{4,5},{5,6},{6,7},{7,8},{8,9},{9,10},{10,1... | collective-permute-start | bytes 196616 | tf_op jit(solution)/shard_map/ppermute | solution.py:31
  3.8 17.3 %collective-permute-start.5 = (f32[2,16,512]{2,1,0:T(8,128)}, f32[2,16,512]{2,1,0:T(8,128)S(1)}, u32[]{:S(2)}, u32[]{:S(2)}) collective-permute-start(f32[2,16,512]{2,1,0:T(8,128)} %own.1), channel_id=1, source_target_pairs={{0,63},{1,0},{2,1},{3,2},{4,3},{5,4},{6,5},{7,6},{8,7},{9,8},{10,9... | collective-permute-start | bytes 196616 | tf_op jit(solution)/shard_map/ppermute | solution.py:31
  21.2 3.6 %collective-permute-start.7 = (f32[2,16,512]{2,1,0:T(8,128)}, f32[2,16,512]{2,1,0:T(8,128)S(1)}, u32[]{:S(2)}, u32[]{:S(2)}) collective-permute-start(f32[2,16,512]{2,1,0:T(8,128)} %vown), channel_id=1, source_target_pairs={{0,63},{1,0},{2,1},{3,2},{4,3},{5,4},{6,5},{7,6},{8,7},{9,8},{10,9... | collective-permute-start | bytes 196616 | tf_op jit(solution)/shard_map/ppermute | solution.py:31
  24.7 0.8 copy-done
  25.6 1.4 %shard_map.126 = (f32[8,32,512]{2,1,0:T(8,128)S(1)}, f32[64,128]{1,0:T(8,128)}, f32[2,32,512]{2,1,0:T(8,128)S(1)}) custom-call(f32[2,16,512]{2,1,0:T(8,128)S(1)} %collective-permute-done.4.prev, f32[2,16,512]{2,1,0:T(8,128)S(1)} %copy-done, f32[2,16,512]{2,1,0:T(8,128)S(1)} %collective-permute-done.5.later), custom_call_target="tpu_custom_call" | custom-call | tf_op jit(solution)/shard_map/pallas_call | solution.py:613
  27.0 15.7 %all-to-all-start.3 = ((f32[64,1,128]{2,1,0:T(1,128)}), f32[64,1,128]{2,1,0:T(1,128)S(1)}, u32[]{:S(2)}, u32[]{:S(2)}) async-start(f32[64,1,128]{2,1,0:T(1,128)} %bitcast.3), calls=%async_computation.3 | async-start | bytes 65536 | tf_op jit(solution)/shard_map/all_to_all | solution.py:622
  42.7 0.7 reverse_bitcast_fusion.3
  43.5 0.7 copy-done.4
  44.2 0.7 pad_maximum_fusion.3.out_taps
  46.1 0.7 pad_maximum_fusion.2.wide_back
  46.9 0.6 pad.32.narrow
  48.3 0.7 pad_maximum_fusion.1.wide
  49.0 0.7 copy-done.5
  49.7 0.7 broadcast_in_dim.15.bias
  50.4 7.9 %shard_map.128 = (bf16[832,512]{1,0:T(8,128)(2,1)}, bf16[832,512]{1,0:T(8,128)(2,1)}, bf16[768,512]{1,0:T(8,128)(2,1)}, bf16[768,512]{1,0:T(8,128)(2,1)}, bf16[7...) custom-call(f32[2,16,512]{2,1,0:T(8,128)} %copy-done.3, ...), custom_call_target="tpu_custom_call" | custom-call | tf_op jit(solution)/shard_map/pallas_call | solution.py:644
  58.3 6.3 %all-to-all-done.3 = f32[64,1,128]{2,1,0:T(1,128)S(1)} async-done(((f32[64,1,128]{2,1,0:T(1,128)}), f32[64,1,128]{2,1,0:T(1,128)S(1)}, u32[]{:S(2)}, u32[]{:S(2)}) %all-to-all-start.3) | async-done | bytes 32800 | tf_op jit(solution)/shard_map/all_to_all | solution.py:622
  64.6 1.0 shard_map.127
  66.5 12.7 %shard_map.129 = (f32[2,16,512]{2,1,0:T(8,128)}, f32[160,128]{1,0:T(8,128)}) custom-call(f32[1,1]{1,0:T(1,128)} %constant.5.clone.1.factor, f32[32,512]{1,0:T(8,128)S(1)} %get-tuple-element.229.pressure, f32[2,32,512]{2,1,0:T(8,128)S(1)} %get-tuple-element.71.around, f32[2,16,512]{2,1,0:T(8,128)} %copy-done.3, f32[2,16,512]{2,1,0:T(8,128)} %vown, ...), custom_call_target="tpu_custom_call" | custom-call | tf_op jit(solution)/shard_map/pallas_call | solution.py:671
  79.2 0.9 reshape.78
  80.1 9.3 %all_to_all.38 = f32[8,20,128]{2,1,0:T(8,128)S(1)} all-to-all(f32[8,20,128]{2,1,0:T(8,128)S(1)} %reshape.78), channel_id=1, replica_groups=mesh['groups'=4,'gx_far'=8,'gx_near'=4,'gx_core'=2] {'gx_near','gx_core'}, dimensions={0} | all-to-all | bytes 163840 | tf_op jit(solution)/shard_map/all_to_all | solution.py:565
  89.4 36.9 %all_to_all.39 = f32[8,20,128]{2,1,0:T(8,128)S(1)} all-to-all(f32[8,20,128]{2,1,0:T(8,128)S(1)} %broadcast_in_dim.16), channel_id=1, replica_groups=mesh['groups'=4,'gx_far'=8,'gx_near'=4,'gx_core'=2] {'gx_far'}, dimensions={0} | all-to-all | bytes 163840 | tf_op jit(solution)/shard_map/all_to_all | solution.py:25
  126.4 13.2 %all_to_all.40 = f32[8,20,128]{2,1,0:T(8,128)S(1)} all-to-all(f32[8,20,128]{2,1,0:T(8,128)S(1)} %broadcast_in_dim.17), channel_id=1, replica_groups=mesh['groups'=4,'gx_far'=8,'gx_near'=4,'gx_core'=2] {'gx_near','gx_core'}, dimensions={0} | all-to-all | bytes 163840 | tf_op jit(solution)/shard_map/all_to_all | solution.py:25
  139.6 0.7 reshape.79.total
  140.2 1.7 %shard_map.130 = (f32[3,3,2,32]{3,2,1,0:T(2,128)}, f32[1,32]{1,0:T(1,128)}, f32[2,3,3,32,32]{4,3,2,1,0:T(8,128)}, f32[2,32]{1,0:T(2,128)}, f32[3,3,2,32]{3,2,1,0:T(2,128)}, /*index=5*/f32[1,2]{1,0:T(1,128)}) custom-call(f32[160,128]{1,0:T(8,128)} %reshape.79.total), custom_call_target="tpu_custom_call" | custom-call | tf_op jit(solution)/shard_map/pallas_call | solution.py:687
  (47 shorter events, 2.4 us)
Async XLA Ops:
  0.6 24.1 %collective-permute-start.4 = (f32[2,16,512]{2,1,0:T(8,128)}, f32[2,16,512]{2,1,0:T(8,128)S(1)}, u32[]{:S(2)}, u32[]{:S(2)}) collective-permute-start(f32[2,16,512]{2,1,0:T(8,128)} %own.1), channel_id=1, source_target_pairs={{0,1},{1,2},{2,3},{3,4},{4,5},{5,6},{6,7},{7,8},{8,9},{9,10},{10,1... | collective-permute-start | bytes 196616 | tf_op jit(solution)/shard_map/ppermute | solution.py:31
  3.8 20.9 %collective-permute-start.5 = (f32[2,16,512]{2,1,0:T(8,128)}, f32[2,16,512]{2,1,0:T(8,128)S(1)}, u32[]{:S(2)}, u32[]{:S(2)}) collective-permute-start(f32[2,16,512]{2,1,0:T(8,128)} %own.1), channel_id=1, source_target_pairs={{0,63},{1,0},{2,1},{3,2},{4,3},{5,4},{6,5},{7,6},{8,7},{9,8},{10,9... | collective-permute-start | bytes 196616 | tf_op jit(solution)/shard_map/ppermute | solution.py:31
  21.2 28.5 %collective-permute-start.7 = (f32[2,16,512]{2,1,0:T(8,128)}, f32[2,16,512]{2,1,0:T(8,128)S(1)}, u32[]{:S(2)}, u32[]{:S(2)}) collective-permute-start(f32[2,16,512]{2,1,0:T(8,128)} %vown), channel_id=1, source_target_pairs={{0,63},{1,0},{2,1},{3,2},{4,3},{5,4},{6,5},{7,6},{8,7},{9,8},{10,9... | collective-permute-start | bytes 196616 | tf_op jit(solution)/shard_map/ppermute | solution.py:31
  24.7 25.0 %collective-permute-start.6 = (f32[2,16,512]{2,1,0:T(8,128)}, f32[2,16,512]{2,1,0:T(8,128)S(1)}, u32[]{:S(2)}, u32[]{:S(2)}) collective-permute-start(f32[2,16,512]{2,1,0:T(8,128)} %vown), channel_id=1, source_target_pairs={{0,1},{1,2},{2,3},{3,4},{4,5},{5,6},{6,7},{7,8},{8,9},{9,10},{10,1... | collective-permute-start | bytes 196616 | tf_op jit(solution)/shard_map/ppermute | solution.py:31
  24.7 0.8 copy-start
  25.6 19.4 %copy-start.1 = (f32[2,3,3,32,32]{4,3,2,1,0:T(8,128)S(1)}, f32[2,3,3,32,32]{4,3,2,1,0:T(8,128)}, u32[]{:S(2)}) copy-start(f32[2,3,3,32,32]{4,3,2,1,0:T(8,128)} %param.15) | copy-start | bytes 221188
  27.0 37.5 %all-to-all-start.3 = ((f32[64,1,128]{2,1,0:T(1,128)}), f32[64,1,128]{2,1,0:T(1,128)S(1)}, u32[]{:S(2)}, u32[]{:S(2)}) async-start(f32[64,1,128]{2,1,0:T(1,128)} %bitcast.3), calls=%async_computation.3 | async-start | bytes 65536 | tf_op jit(solution)/shard_map/all_to_all | solution.py:622
  43.5 0.7 copy-start.4
  49.0 0.7 copy-start.5
  49.0 0.7 copy-start.6
  49.7 0.7 copy-start.2
  49.7 0.7 copy-start.3

commit v4 on v3

--- a/solution.py
+++ b/solution.py
@@ -215,9 +215,8 @@
 
 def banded_narrow(taps):
     rows = jnp.concatenate([taps] + [turn(taps, r, 1) for r in range(1, BLOCK)], axis=0)
-    high = rows.astype(BF16).astype(F32)
-    low = rows - high
-    return (high + turn(high, 16, 1) + turn(low, 32, 1)).astype(BF16)[:, :48]
+    high, low = halves(rows)
+    return jnp.concatenate([high[:, :48], high[:, :48], low[:, :48]], axis=1)
 
 
 def banded_out(taps, rows):
@@ -247,10 +246,11 @@
 
 
 def narrow_conv(weights, pair):
-    high, low = halves(jnp.concatenate(pair, axis=0))
+    x = jnp.concatenate(pair, axis=0)
+    high, low = halves(jnp.concatenate([turn(x, 1, 1), x, turn(x, -1, 1)], axis=0))
     x = jnp.concatenate([high, low, high], axis=0)
     y = jnp.dot(weights, x, preferred_element_type=F32)
-    return side_sum(y.reshape(BLOCK, 96, y.shape[1]))
+    return y.reshape(BLOCK, 32, y.shape[1])
 
 
 def put(refs, at, value):
@@ -382,6 +382,8 @@
     e0,
     eh,
     el,
+    fh,
+    fl,
     band2,
     a2h,
     a2l,
@@ -396,6 +398,7 @@
 ):
     rows, width = vown.shape[1], vown.shape[2]
     a0, a1, a2, split = (a0h, a0l), (a1h, a1l), (a2h, a2l), (eh, el)
+    other = (fh, fl)
     sources = (far2, far2h, far2l, far1, far1h, far1l, far0, far0h, far0l, far_out)
     targets = (band2, a2h, a2l, band1, a1h, a1l, band0, a0h, a0l, band_out)
     copies = [
@@ -415,37 +418,29 @@
         a = high.astype(F32) + low.astype(F32)
         return (1.0 - a * a).reshape(BLOCK, 32, width)
 
-    def keep(ref, at, value):
-        put(split, at, value)
+    def keep(ref, parts, at, value):
+        put(parts, at, value)
         ref[pl.ds(at * 32, BLOCK * 32), :] = value.reshape(BLOCK * 32, width)
 
     for copy in copies[:3]:
         copy.wait()
     for s in starts(-3, rows + 6):
         pair = [e3[c][s + 7 : s + 7 + SPAN] for c in range(2)]
-        keep(e2, s + 3, narrow_conv(band2[...], pair) * slope_of(a2, s + 3))
+        keep(e2, split, s + 3, narrow_conv(band2[...], pair) * slope_of(a2, s + 3))
     for copy in copies[3:6]:
         copy.wait()
     for s in starts(-2, rows + 4):
         x = take(split, s + 2, SPAN)
-        e1[pl.ds((s + 2) * 32, BLOCK * 32), :] = (
-            wide_conv(band1[...], *x) * slope_of(a1, s + 4)
-        ).reshape(BLOCK * 32, width)
-    split_rows = (rows + 4) * 32
-    high, low = halves(e1[...])
-    eh[0:split_rows, :] = high
-    el[0:split_rows, :] = low
+        keep(e1, other, s + 2, wide_conv(band1[...], *x) * slope_of(a1, s + 4))
     for copy in copies[6:]:
         copy.wait()
     for s in starts(-1, rows + 2):
-        x = take(split, s + 1, SPAN)
-        e0[pl.ds((s + 1) * 32, BLOCK * 32), :] = (
-            wide_conv(band0[...], *x) * slope_of(a0, s + 5)
-        ).reshape(BLOCK * 32, width)
+        x = take(other, s + 1, SPAN)
+        keep(e0, split, s + 1, wide_conv(band0[...], *x) * slope_of(a0, s + 5))
 
     own = slice(8, 8 + rows)
-    high, low = halves(e0[...])
     cells = (rows + 2) * 32
+    high, low = eh[0:cells, :], el[0:cells, :]
     wh, wl = band_out[0, :, :cells], band_out[1, :, :cells]
     y = (
         jnp.dot(wh, high, preferred_element_type=F32)
@@ -520,42 +515,25 @@
         ends = ends + jnp.where(lane == 96 + c, end, 0.0)
     sums = [bias_line(e2, 3, rows), bias_line(e1, 2, rows), bias_line(e0, 1, rows), ends]
     sums = eight_rows(jnp.concatenate(sums, axis=0))
-    place = lax.broadcasted_iota(jnp.int32, (8, 128), 1) // 32
-
-    def merged(parts, rest):
-        for p, part in enumerate(parts):
-            rest = jnp.where(place == p, part, rest)
-        return rest
-
-    terms[0:72, :] = dense(middle1) * scale
-    terms[72:144, :] = dense(middle0) * scale
-    terms[144:152, :] = merged(last, sums) * scale
-    terms[152:160, :] = merged(begin, jnp.zeros_like(sums)) * scale
-
-
-def dense(x):
-    flat = jnp.concatenate([x[:, 32 * p : 32 * p + 32] for p in range(3)], axis=0)
-    return jnp.concatenate([flat[72 * g : 72 * g + 72] for g in range(4)], axis=1)
-
-
-def sparse(x):
-    flat = jnp.concatenate([x[:, 32 * g : 32 * g + 32] for g in range(4)], axis=0)
-    return [flat[96 * p : 96 * p + 96] for p in range(3)]
+    kept = lax.broadcasted_iota(jnp.int32, (96, 128), 1) < 96
+    rest = jnp.concatenate(last + begin + [sums, jnp.zeros((40, 128), F32)], axis=0)
+    terms[0:96, :] = jnp.where(kept, middle1, rest) * scale
+    terms[96:192, :] = jnp.where(kept, middle0, 0.0) * scale
 
 
 def unpack_kernel(total, first, bias0, hidden, biases, last, ends):
-    for at, begin in enumerate((72, 0)):
-        for p, block in enumerate(sparse(total[begin : begin + 72, :])):
-            hidden[at, p] = block.reshape(3, 32, 32)
     for p in range(3):
-        for ref, begin in ((last, 144), (first, 152)):
-            part = total[begin : begin + 8, 32 * p : 32 * p + 32]
+        for at, begin in enumerate((96, 0)):
+            hidden[at, p] = total[begin : begin + 96, 32 * p : 32 * p + 32].reshape(3, 32, 32)
+    rest = turn(total[0:56, :], 32, 1)[:, :32]
+    for p in range(3):
+        for ref, begin in ((last, 8 * p), (first, 24 + 8 * p)):
             for q in range(3):
-                ref[p, q] = jnp.concatenate([part[q : q + 1], part[3 + q : 4 + q]], axis=0)
-    sums = total[144:152, 96:128]
-    biases[...] = jnp.concatenate([sums[1:2], sums[0:1]], axis=0)
-    bias0[...] = sums[2:3]
-    ends[...] = sums[3:4, :2]
+                at = begin + q
+                ref[p, q] = jnp.concatenate([rest[at : at + 1], rest[at + 3 : at + 4]], axis=0)
+    biases[...] = jnp.concatenate([rest[49:50], rest[48:49]], axis=0)
+    bias0[...] = rest[50:51]
+    ends[...] = rest[51:52, :2]
 
 
 def total_of(packed):
@@ -578,9 +556,9 @@
 
 
 def narrow_taps(w):
-    t = jnp.transpose(w, (1, 2, 3, 0)).reshape(3 * w.shape[2], 2, 3)
-    t = jnp.pad(t, ((0, 0), (0, 0), (0, 5))).reshape(-1, 16)
-    return jnp.pad(t, ((0, 0), (0, 112)))
+    t = jnp.transpose(w, (2, 1, 3, 0))
+    t = jnp.pad(t, ((0, 0), (0, 0), (0, 0), (0, 5))).reshape(w.shape[2], 48)
+    return jnp.pad(t, ((0, 0), (0, 80)))
 
 
 def out_taps_of(w):
@@ -638,7 +616,7 @@
     heights = (rows + 10, rows + 8, rows + 6)
     held = [shape_of(h * 32, width, dtype=BF16) for h in heights for _ in range(2)]
     wide_band = shape_of(96 * BLOCK, 3 * SPAN * 32, dtype=BF16)
-    narrow_band = shape_of(96 * BLOCK, 48, dtype=BF16)
+    narrow_band = shape_of(32 * BLOCK, 144, dtype=BF16)
     edge = -(-(rows + 2) * 32 // 128) * 128
     held += [narrow_band, wide_band, wide_band, shape_of(2, 6 * rows, edge, dtype=BF16)]
     a0h, a0l, a1h, a1l, a2h, a2l, band2, band1, band0, band_out = call(
@@ -670,13 +648,15 @@
     fetched = (band2, a2h, a2l, band1, a1h, a1l, band0, a0h, a0l, band_out)
     grad_velocity, terms = call(
         backward_kernel,
-        (shape_of(2, rows, width), shape_of(160, 128)),
+        (shape_of(2, rows, width), shape_of(192, 128)),
         [
             pltpu.VMEM(((rows + 6) * 32, width), F32),
             pltpu.VMEM(((rows + 4) * 32, width), F32),
             pltpu.VMEM(((rows + 2) * 32, width), F32),
             pltpu.VMEM(((rows + 6) * 32, width), BF16),
             pltpu.VMEM(((rows + 6) * 32, width), BF16),
+            pltpu.VMEM(((rows + 4) * 32, width), BF16),
+            pltpu.VMEM(((rows + 4) * 32, width), BF16),
         ]
         + [pltpu.VMEM(item.shape, item.dtype) for item in fetched]
         + [pltpu.SemaphoreType.DMA((len(fetched),))],

time: 143 us -> 142 us (level)
  local copies, waits for them, and re-layouts: 7.94 us -> 6.24 us
    reshape x6 -> x2, local copies, waits for them, and re-layouts: 1.74 us -> 0.14 us  [narrow_taps(): t = jnp.pad(t, ((0, 0), (0, 0), (0, 0), (0, 5))).reshape(w.shape[2], 48)]
where the time goes in v4:
time: 142 us; the launch traced here: 141 us
  blocking collectives  60.3 us (42%)
  starting transfers between devices  39.8 us (28%)
  Pallas kernels  24.6 us (17%)
  waiting for transfers between devices  6.39 us (4%)
  local copies, waits for them, and re-layouts  6.24 us (4%)
  other arithmetic  2.08 us (1%)
  between operations  1.46 us (1%)
    all_to_all x2, blocking collectives, from_everyone(): lax.all_to_all(jnp.broadcast_to(x[None], (length, *x.shape)), axis, 0, 0,...  50.1 us
    ppermute x4, starting transfers between devices, shifted(): return lax.ppermute(value, axis, pairs)  24.1 us
    all_to_all x1, starting transfers between devices, body(): lax.all_to_all(sums.reshape(members, 1, 128), GX, 0, 0, tiled=True)  15.7 us
    pallas_call x1, Pallas kernels, body(): call(backward_kernel, (shape_of(2, rows, width), shape_of(192, 128)), [pl...  12.5 us
    all_to_all x1, blocking collectives, total_of(): part = lax.all_to_all(part, local, 0, 0, tiled=True).sum(axis=0)  10.2 us
    pallas_call x1, Pallas kernels, body(): call(forward_kernel, tuple(held), [pltpu.VMEM(item.shape, item.dtype) for...  7.88 us
    all_to_all x1, waiting for transfers between devices, body(): lax.all_to_all(sums.reshape(members, 1, 128), GX, 0, 0, tiled=True)  6.38 us
  transfers between devices with their start and end apart: 5, of which 1 were waited for; matrix products, arithmetic and copies ran while one was open for 4% of the time, Pallas kernels for 7%

profile of v4, /device:TPU:37, one launch (start us, length us, event | category | flops | bytes accessed | tf_op | source)
XLA Modules:
  0.0 141.1 jit_solution(17256662301519685363)
XLA Ops:
  0.6 3.2 %collective-permute-start.4 = (f32[2,16,512]{2,1,0:T(8,128)}, f32[2,16,512]{2,1,0:T(8,128)S(1)}, u32[]{:S(2)}, u32[]{:S(2)}) collective-permute-start(f32[2,16,512]{2,1,0:T(8,128)} %own.1), channel_id=1, source_target_pairs={{0,1},{1,2},{2,3},{3,4},{4,5},{5,6},{6,7},{7,8},{8,9},{9,10},{10,1... | collective-permute-start | bytes 196616 | tf_op jit(solution)/shard_map/ppermute | solution.py:31
  3.8 17.3 %collective-permute-start.5 = (f32[2,16,512]{2,1,0:T(8,128)}, f32[2,16,512]{2,1,0:T(8,128)S(1)}, u32[]{:S(2)}, u32[]{:S(2)}) collective-permute-start(f32[2,16,512]{2,1,0:T(8,128)} %own.1), channel_id=1, source_target_pairs={{0,63},{1,0},{2,1},{3,2},{4,3},{5,4},{6,5},{7,6},{8,7},{9,8},{10,9... | collective-permute-start | bytes 196616 | tf_op jit(solution)/shard_map/ppermute | solution.py:31
  21.2 3.6 %collective-permute-start.7 = (f32[2,16,512]{2,1,0:T(8,128)}, f32[2,16,512]{2,1,0:T(8,128)S(1)}, u32[]{:S(2)}, u32[]{:S(2)}) collective-permute-start(f32[2,16,512]{2,1,0:T(8,128)} %vown), channel_id=1, source_target_pairs={{0,63},{1,0},{2,1},{3,2},{4,3},{5,4},{6,5},{7,6},{8,7},{9,8},{10,9... | collective-permute-start | bytes 196616 | tf_op jit(solution)/shard_map/ppermute | solution.py:31
  24.7 0.8 copy-done
  25.6 1.4 %shard_map.126 = (f32[8,32,512]{2,1,0:T(8,128)S(1)}, f32[64,128]{1,0:T(8,128)}, f32[2,32,512]{2,1,0:T(8,128)S(1)}) custom-call(f32[2,16,512]{2,1,0:T(8,128)S(1)} %collective-permute-done.4.prev, f32[2,16,512]{2,1,0:T(8,128)S(1)} %copy-done, f32[2,16,512]{2,1,0:T(8,128)S(1)} %collective-permute-done.5.later), custom_call_target="tpu_custom_call" | custom-call | tf_op jit(solution)/shard_map/pallas_call | solution.py:591
  27.0 15.7 %all-to-all-start.3 = ((f32[64,1,128]{2,1,0:T(1,128)}), f32[64,1,128]{2,1,0:T(1,128)S(1)}, u32[]{:S(2)}, u32[]{:S(2)}) async-start(f32[64,1,128]{2,1,0:T(1,128)} %bitcast.3), calls=%async_computation.3 | async-start | bytes 65536 | tf_op jit(solution)/shard_map/all_to_all | solution.py:600
  42.7 0.7 reverse_bitcast_fusion.2
  43.4 0.7 pad_maximum_fusion.3.out_taps
  45.2 0.7 pad_maximum_fusion.2.wide_back
  45.9 0.7 copy-done.5
  46.7 0.6 pad.36.narrow_back
  47.5 0.6 pad.32.narrow
  48.1 0.7 pad_maximum_fusion.1.wide
  48.8 0.7 copy-done.6
  49.5 0.7 broadcast_in_dim.15.bias
  50.3 7.9 %shard_map.128 = (bf16[832,512]{1,0:T(8,128)(2,1)}, bf16[832,512]{1,0:T(8,128)(2,1)}, bf16[768,512]{1,0:T(8,128)(2,1)}, bf16[768,512]{1,0:T(8,128)(2,1)}, bf16[7...) custom-call(f32[2,16,512]{2,1,0:T(8,128)} %copy-done.3, ...), custom_call_target="tpu_custom_call" | custom-call | tf_op jit(solution)/shard_map/pallas_call | solution.py:622
  58.1 6.4 %all-to-all-done.3 = f32[64,1,128]{2,1,0:T(1,128)S(1)} async-done(((f32[64,1,128]{2,1,0:T(1,128)}), f32[64,1,128]{2,1,0:T(1,128)S(1)}, u32[]{:S(2)}, u32[]{:S(2)}) %all-to-all-start.3) | async-done | bytes 32800 | tf_op jit(solution)/shard_map/all_to_all | solution.py:600
  64.5 1.0 shard_map.127
  66.2 0.2 conditional.1
  66.4 12.5 %shard_map.129 = (f32[2,16,512]{2,1,0:T(8,128)}, f32[192,128]{1,0:T(8,128)}) custom-call(f32[1,1]{1,0:T(1,128)} %constant.5.clone.1.factor, f32[32,512]{1,0:T(8,128)S(1)} %get-tuple-element.229.pressure, f32[2,32,512]{2,1,0:T(8,128)S(1)} %get-tuple-element.71.around, f32[2,16,512]{2,1,0:T(8,128)} %copy-done.3, f32[2,16,512]{2,1,0:T(8,128)} %vown, ...), custom_call_target="tpu_custom_call" | custom-call | tf_op jit(solution)/shard_map/pallas_call | solution.py:649
  79.0 10.2 %all_to_all.38 = f32[8,24,128]{2,1,0:T(8,128)S(1)} all-to-all(f32[8,24,128]{2,1,0:T(8,128)} %bitcast.50), channel_id=1, replica_groups=mesh['groups'=4,'gx_far'=8,'gx_near'=4,'gx_core'=2] {'gx_near','gx_core'}, dimensions={0} | all-to-all | bytes 196608 | tf_op jit(solution)/shard_map/all_to_all | solution.py:543
  89.2 36.8 %all_to_all.39 = f32[8,24,128]{2,1,0:T(8,128)S(1)} all-to-all(f32[8,24,128]{2,1,0:T(8,128)S(1)} %broadcast_in_dim.16), channel_id=1, replica_groups=mesh['groups'=4,'gx_far'=8,'gx_near'=4,'gx_core'=2] {'gx_far'}, dimensions={0} | all-to-all | bytes 196608 | tf_op jit(solution)/shard_map/all_to_all | solution.py:25
  126.0 13.3 %all_to_all.40 = f32[8,24,128]{2,1,0:T(8,128)} all-to-all(f32[8,24,128]{2,1,0:T(8,128)S(1)} %broadcast_in_dim.17), channel_id=1, replica_groups=mesh['groups'=4,'gx_far'=8,'gx_near'=4,'gx_core'=2] {'gx_near','gx_core'}, dimensions={0} | all-to-all | bytes 196608 | tf_op jit(solution)/shard_map/all_to_all | solution.py:25
  139.3 1.7 %shard_map.130 = (f32[3,3,2,32]{3,2,1,0:T(2,128)}, f32[1,32]{1,0:T(1,128)}, f32[2,3,3,32,32]{4,3,2,1,0:T(8,128)}, f32[2,32]{1,0:T(2,128)}, f32[3,3,2,32]{3,2,1,0:T(2,128)}, /*index=5*/f32[1,2]{1,0:T(1,128)}) custom-call(f32[192,128]{1,0:T(8,128)} %bitcast.49), custom_call_target="tpu_custom_call" | custom-call | tf_op jit(solution)/shard_map/pallas_call | solution.py:667
  (45 shorter events, 1.5 us)
Async XLA Ops:
  0.6 24.1 %collective-permute-start.4 = (f32[2,16,512]{2,1,0:T(8,128)}, f32[2,16,512]{2,1,0:T(8,128)S(1)}, u32[]{:S(2)}, u32[]{:S(2)}) collective-permute-start(f32[2,16,512]{2,1,0:T(8,128)} %own.1), channel_id=1, source_target_pairs={{0,1},{1,2},{2,3},{3,4},{4,5},{5,6},{6,7},{7,8},{8,9},{9,10},{10,1... | collective-permute-start | bytes 196616 | tf_op jit(solution)/shard_map/ppermute | solution.py:31
  3.8 20.9 %collective-permute-start.5 = (f32[2,16,512]{2,1,0:T(8,128)}, f32[2,16,512]{2,1,0:T(8,128)S(1)}, u32[]{:S(2)}, u32[]{:S(2)}) collective-permute-start(f32[2,16,512]{2,1,0:T(8,128)} %own.1), channel_id=1, source_target_pairs={{0,63},{1,0},{2,1},{3,2},{4,3},{5,4},{6,5},{7,6},{8,7},{9,8},{10,9... | collective-permute-start | bytes 196616 | tf_op jit(solution)/shard_map/ppermute | solution.py:31
  21.2 28.3 %collective-permute-start.7 = (f32[2,16,512]{2,1,0:T(8,128)}, f32[2,16,512]{2,1,0:T(8,128)S(1)}, u32[]{:S(2)}, u32[]{:S(2)}) collective-permute-start(f32[2,16,512]{2,1,0:T(8,128)} %vown), channel_id=1, source_target_pairs={{0,63},{1,0},{2,1},{3,2},{4,3},{5,4},{6,5},{7,6},{8,7},{9,8},{10,9... | collective-permute-start | bytes 196616 | tf_op jit(solution)/shard_map/ppermute | solution.py:31
  24.7 24.8 %collective-permute-start.6 = (f32[2,16,512]{2,1,0:T(8,128)}, f32[2,16,512]{2,1,0:T(8,128)S(1)}, u32[]{:S(2)}, u32[]{:S(2)}) collective-permute-start(f32[2,16,512]{2,1,0:T(8,128)} %vown), channel_id=1, source_target_pairs={{0,1},{1,2},{2,3},{3,4},{4,5},{5,6},{6,7},{7,8},{8,9},{9,10},{10,1... | collective-permute-start | bytes 196616 | tf_op jit(solution)/shard_map/ppermute | solution.py:31
  24.7 0.8 copy-start
  25.6 18.5 %copy-start.1 = (f32[2,3,3,32,32]{4,3,2,1,0:T(8,128)S(1)}, f32[2,3,3,32,32]{4,3,2,1,0:T(8,128)}, u32[]{:S(2)}) copy-start(f32[2,3,3,32,32]{4,3,2,1,0:T(8,128)} %param.15) | copy-start | bytes 221188
  27.0 37.5 %all-to-all-start.3 = ((f32[64,1,128]{2,1,0:T(1,128)}), f32[64,1,128]{2,1,0:T(1,128)S(1)}, u32[]{:S(2)}, u32[]{:S(2)}) async-start(f32[64,1,128]{2,1,0:T(1,128)} %bitcast.3), calls=%async_computation.3 | async-start | bytes 65536 | tf_op jit(solution)/shard_map/all_to_all | solution.py:600
  45.9 0.7 copy-start.5
  46.7 0.7 copy-start.4
  48.8 0.7 copy-start.6
  48.8 0.7 copy-start.7
  49.5 0.7 copy-start.2
  49.5 0.7 copy-start.3

commit v5 on v4

--- a/solution.py
+++ b/solution.py
@@ -253,15 +253,27 @@
     return y.reshape(BLOCK, 32, y.shape[1])
 
 
+def rows_at(at, rows):
+    return pl.ds(at * 32 if isinstance(at, int) else pl.multiple_of(at * 32, 32), rows * 32)
+
+
+def each_block(first, count, visit):
+    def step(i, _):
+        visit(first + jnp.minimum(BLOCK * i, count - BLOCK))
+        return 0
+
+    lax.fori_loop(0, -(-count // BLOCK), step, 0)
+
+
 def put(refs, at, value):
     high, low = halves(value.reshape(value.shape[0] * 32, value.shape[2]))
-    span = pl.ds(at * 32, value.shape[0] * 32)
+    span = rows_at(at, value.shape[0])
     refs[0][span, :] = high
     refs[1][span, :] = low
 
 
 def take(refs, at, rows):
-    span = pl.ds(at * 32, rows * 32)
+    span = rows_at(at, rows)
     return refs[0][span, :], refs[1][span, :]
 
 
@@ -320,21 +332,23 @@
     return jnp.concatenate([turn(e, -1, e.ndim - 1), e, turn(e, 1, e.ndim - 1)], axis=axis)
 
 
-def wide_terms(err, err_at, act, act_at, rows):
-    total = None
-    lines = -(-rows // BLOCK)
-    for i in range(lines):
-        s = min(BLOCK * i, rows - BLOCK)
-        e = err[pl.ds((err_at + s) * 32, BLOCK * 32), :].reshape(BLOCK, 32, -1)
-        spent = BLOCK * i - s
-        if spent:
-            e = jnp.concatenate([jnp.zeros_like(e[:spent]), e[spent:]], axis=0)
+def wide_terms(err, err_at, act, act_at, rows, held):
+    held[...] = jnp.zeros_like(held)
+
+    def step(i, _):
+        s = jnp.minimum(BLOCK * i, rows - BLOCK)
+        e = err[rows_at(err_at + s, BLOCK), :].reshape(BLOCK, 32, -1)
+        line = lax.broadcasted_iota(jnp.int32, e.shape, 0)
+        e = jnp.where(line >= BLOCK * i - s, e, 0.0)
         high, low = halves(sided(e, 1).reshape(BLOCK * 96, -1))
         ah, al = take(act, act_at + s - 1, SPAN)
-        term = dot_nt(
+        held[...] += dot_nt(
             jnp.concatenate([high, high, low], axis=1), jnp.concatenate([ah, al, ah], axis=1)
         )
-        total = term if total is None else total + term
+        return 0
+
+    lax.fori_loop(0, -(-rows // BLOCK), step, 0)
+    total = held[...]
     total = total.reshape(BLOCK, 96, SPAN * 32)
     out = None
     for r in range(BLOCK):
@@ -384,6 +398,7 @@
     el,
     fh,
     fl,
+    held,
     band2,
     a2h,
     a2l,
@@ -420,7 +435,7 @@
 
     def keep(ref, parts, at, value):
         put(parts, at, value)
-        ref[pl.ds(at * 32, BLOCK * 32), :] = value.reshape(BLOCK * 32, width)
+        ref[rows_at(at, BLOCK), :] = value.reshape(BLOCK * 32, width)
 
     for copy in copies[:3]:
         copy.wait()
@@ -429,14 +444,20 @@
         keep(e2, split, s + 3, narrow_conv(band2[...], pair) * slope_of(a2, s + 3))
     for copy in copies[3:6]:
         copy.wait()
-    for s in starts(-2, rows + 4):
+
+    def middle(s):
         x = take(split, s + 2, SPAN)
         keep(e1, other, s + 2, wide_conv(band1[...], *x) * slope_of(a1, s + 4))
+
+    each_block(-2, rows + 4, middle)
     for copy in copies[6:]:
         copy.wait()
-    for s in starts(-1, rows + 2):
+
+    def foremost(s):
         x = take(other, s + 1, SPAN)
         keep(e0, split, s + 1, wide_conv(band0[...], *x) * slope_of(a0, s + 5))
+
+    each_block(-1, rows + 2, foremost)
 
     own = slice(8, 8 + rows)
     cells = (rows + 2) * 32
@@ -470,8 +491,8 @@
         grad_velocity[k] = adjoint[k][own] - step_size * (direct[k] - cross[k]) + through[k]
 
     scale = factor[0, 0]
-    middle1 = wide_terms(e2, 3, a1, 4, rows)
-    middle0 = wide_terms(e1, 2, a0, 5, rows)
+    middle1 = wide_terms(e2, 3, a1, 4, rows, held)
+    middle0 = wide_terms(e1, 2, a0, 5, rows, held)
 
     outer = jnp.concatenate([sided(e3[c][own], 0) for c in range(2)], axis=0)
     lh, ll = halves(outer)
@@ -657,6 +678,7 @@
             pltpu.VMEM(((rows + 6) * 32, width), BF16),
             pltpu.VMEM(((rows + 4) * 32, width), BF16),
             pltpu.VMEM(((rows + 4) * 32, width), BF16),
+            pltpu.VMEM((BLOCK * 96, SPAN * 32), F32),
         ]
         + [pltpu.VMEM(item.shape, item.dtype) for item in fetched]
         + [pltpu.SemaphoreType.DMA((len(fetched),))],

time: 142 us -> 145 us (1.021)
  Pallas kernels: 24.6 us -> 27.7 us
    pallas_call x1, Pallas kernels: 12.5 us -> 15.7 us  [body(): call(backward_kernel, (shape_of(2, rows, width), shape_of(192, 128)), [pl...]
  transfers between devices with their start and end apart: 5 -> 5, of which waited for: 1 -> 1; matrix products, arithmetic and copies ran while one was open for 4% -> 4% of each run, Pallas kernels for 7% -> 6%
where the time goes in v5:
time: 145 us; the launch traced here: 144 us
  blocking collectives  60.3 us (42%)
  starting transfers between devices  39.8 us (27%)
  Pallas kernels  27.7 us (19%)
  waiting for transfers between devices  6.39 us (4%)
  local copies, waits for them, and re-layouts  6.24 us (4%)
  other arithmetic  2.08 us (1%)
  between operations  1.46 us (1%)
    all_to_all x2, blocking collectives, from_everyone(): lax.all_to_all(jnp.broadcast_to(x[None], (length, *x.shape)), axis, 0, 0,...  50.1 us
    ppermute x4, starting transfers between devices, shifted(): return lax.ppermute(value, axis, pairs)  24.1 us
    pallas_call x1, Pallas kernels, body(): call(backward_kernel, (shape_of(2, rows, width), shape_of(192, 128)), [pl...  15.7 us
    all_to_all x1, starting transfers between devices, body(): lax.all_to_all(sums.reshape(members, 1, 128), GX, 0, 0, tiled=True)  15.7 us
    all_to_all x1, blocking collectives, total_of(): part = lax.all_to_all(part, local, 0, 0, tiled=True).sum(axis=0)  10.2 us
    pallas_call x1, Pallas kernels, body(): call(forward_kernel, tuple(held), [pltpu.VMEM(item.shape, item.dtype) for...  7.88 us
    all_to_all x1, waiting for transfers between devices, body(): lax.all_to_all(sums.reshape(members, 1, 128), GX, 0, 0, tiled=True)  6.38 us
  transfers between devices with their start and end apart: 5, of which 1 were waited for; matrix products, arithmetic and copies ran while one was open for 4% of the time, Pallas kernels for 6%

profile of v5, /device:TPU:37, one launch (start us, length us, event | category | flops | bytes accessed | tf_op | source)
XLA Modules:
  0.0 144.2 jit_solution(15002968765022884226)
XLA Ops:
  0.6 3.2 %collective-permute-start.4 = (f32[2,16,512]{2,1,0:T(8,128)}, f32[2,16,512]{2,1,0:T(8,128)S(1)}, u32[]{:S(2)}, u32[]{:S(2)}) collective-permute-start(f32[2,16,512]{2,1,0:T(8,128)} %own.1), channel_id=1, source_target_pairs={{0,1},{1,2},{2,3},{3,4},{4,5},{5,6},{6,7},{7,8},{8,9},{9,10},{10,1... | collective-permute-start | bytes 196616 | tf_op jit(solution)/shard_map/ppermute | solution.py:31
  3.8 17.3 %collective-permute-start.5 = (f32[2,16,512]{2,1,0:T(8,128)}, f32[2,16,512]{2,1,0:T(8,128)S(1)}, u32[]{:S(2)}, u32[]{:S(2)}) collective-permute-start(f32[2,16,512]{2,1,0:T(8,128)} %own.1), channel_id=1, source_target_pairs={{0,63},{1,0},{2,1},{3,2},{4,3},{5,4},{6,5},{7,6},{8,7},{9,8},{10,9... | collective-permute-start | bytes 196616 | tf_op jit(solution)/shard_map/ppermute | solution.py:31
  21.2 3.6 %collective-permute-start.7 = (f32[2,16,512]{2,1,0:T(8,128)}, f32[2,16,512]{2,1,0:T(8,128)S(1)}, u32[]{:S(2)}, u32[]{:S(2)}) collective-permute-start(f32[2,16,512]{2,1,0:T(8,128)} %vown), channel_id=1, source_target_pairs={{0,63},{1,0},{2,1},{3,2},{4,3},{5,4},{6,5},{7,6},{8,7},{9,8},{10,9... | collective-permute-start | bytes 196616 | tf_op jit(solution)/shard_map/ppermute | solution.py:31
  24.7 0.8 copy-done
  25.6 1.4 shard_map.126
  27.0 15.7 %all-to-all-start.3 = ((f32[64,1,128]{2,1,0:T(1,128)}), f32[64,1,128]{2,1,0:T(1,128)S(1)}, u32[]{:S(2)}, u32[]{:S(2)}) async-start(f32[64,1,128]{2,1,0:T(1,128)} %bitcast.3), calls=%async_computation.3 | async-start | bytes 65536 | tf_op jit(solution)/shard_map/all_to_all | solution.py:621
  42.7 0.7 reverse_bitcast_fusion.2
  43.4 0.7 pad_maximum_fusion.3.out_taps
  45.2 0.7 pad_maximum_fusion.2.wide_back
  45.9 0.7 copy-done.5
  46.7 0.6 pad.36.narrow_back
  47.5 0.6 pad.32.narrow
  48.1 0.7 pad_maximum_fusion.1.wide
  48.8 0.7 copy-done.6
  49.5 0.7 broadcast_in_dim.15.bias
  50.3 7.9 %shard_map.128 = (bf16[832,512]{1,0:T(8,128)(2,1)}, bf16[832,512]{1,0:T(8,128)(2,1)}, bf16[768,512]{1,0:T(8,128)(2,1)}, bf16[768,512]{1,0:T(8,128)(2,1)}, bf16[7...) custom-call(f32[2,16,512]{2,1,0:T(8,128)} %copy-done.3, ...), custom_call_target="tpu_custom_call" | custom-call | tf_op jit(solution)/shard_map/pallas_call | solution.py:643
  58.1 6.4 %all-to-all-done.3 = f32[64,1,128]{2,1,0:T(1,128)S(1)} async-done(((f32[64,1,128]{2,1,0:T(1,128)}), f32[64,1,128]{2,1,0:T(1,128)S(1)}, u32[]{:S(2)}, u32[]{:S(2)}) %all-to-all-start.3) | async-done | bytes 32800 | tf_op jit(solution)/shard_map/all_to_all | solution.py:621
  64.5 1.0 shard_map.127
  66.2 0.2 conditional.1
  66.4 15.7 %shard_map.129 = (f32[2,16,512]{2,1,0:T(8,128)}, f32[192,128]{1,0:T(8,128)}) custom-call(f32[1,1]{1,0:T(1,128)} %constant.5.clone.1.factor, f32[32,512]{1,0:T(8,128)S(1)} %get-tuple-element.229.pressure, f32[2,32,512]{2,1,0:T(8,128)S(1)} %get-tuple-element.71.around, f32[2,16,512]{2,1,0:T(8,128)} %copy-done.3, f32[2,16,512]{2,1,0:T(8,128)} %vown, ...), custom_call_target="tpu_custom_call" | custom-call | tf_op jit(solution)/shard_map/pallas_call | solution.py:670
  82.1 10.2 %all_to_all.38 = f32[8,24,128]{2,1,0:T(8,128)S(1)} all-to-all(f32[8,24,128]{2,1,0:T(8,128)} %bitcast.50), channel_id=1, replica_groups=mesh['groups'=4,'gx_far'=8,'gx_near'=4,'gx_core'=2] {'gx_near','gx_core'}, dimensions={0} | all-to-all | bytes 196608 | tf_op jit(solution)/shard_map/all_to_all | solution.py:564
  92.3 36.8 %all_to_all.39 = f32[8,24,128]{2,1,0:T(8,128)S(1)} all-to-all(f32[8,24,128]{2,1,0:T(8,128)S(1)} %broadcast_in_dim.16), channel_id=1, replica_groups=mesh['groups'=4,'gx_far'=8,'gx_near'=4,'gx_core'=2] {'gx_far'}, dimensions={0} | all-to-all | bytes 196608 | tf_op jit(solution)/shard_map/all_to_all | solution.py:25
  129.2 13.3 %all_to_all.40 = f32[8,24,128]{2,1,0:T(8,128)} all-to-all(f32[8,24,128]{2,1,0:T(8,128)S(1)} %broadcast_in_dim.17), channel_id=1, replica_groups=mesh['groups'=4,'gx_far'=8,'gx_near'=4,'gx_core'=2] {'gx_near','gx_core'}, dimensions={0} | all-to-all | bytes 196608 | tf_op jit(solution)/shard_map/all_to_all | solution.py:25
  142.5 1.7 %shard_map.130 = (f32[3,3,2,32]{3,2,1,0:T(2,128)}, f32[1,32]{1,0:T(1,128)}, f32[2,3,3,32,32]{4,3,2,1,0:T(8,128)}, f32[2,32]{1,0:T(2,128)}, f32[3,3,2,32]{3,2,1,0:T(2,128)}, /*index=5*/f32[1,2]{1,0:T(1,128)}) custom-call(f32[192,128]{1,0:T(8,128)} %bitcast.49), custom_call_target="tpu_custom_call" | custom-call | tf_op jit(solution)/shard_map/pallas_call | solution.py:689
  (45 shorter events, 1.5 us)
Async XLA Ops:
  0.6 24.1 %collective-permute-start.4 = (f32[2,16,512]{2,1,0:T(8,128)}, f32[2,16,512]{2,1,0:T(8,128)S(1)}, u32[]{:S(2)}, u32[]{:S(2)}) collective-permute-start(f32[2,16,512]{2,1,0:T(8,128)} %own.1), channel_id=1, source_target_pairs={{0,1},{1,2},{2,3},{3,4},{4,5},{5,6},{6,7},{7,8},{8,9},{9,10},{10,1... | collective-permute-start | bytes 196616 | tf_op jit(solution)/shard_map/ppermute | solution.py:31
  3.8 20.9 %collective-permute-start.5 = (f32[2,16,512]{2,1,0:T(8,128)}, f32[2,16,512]{2,1,0:T(8,128)S(1)}, u32[]{:S(2)}, u32[]{:S(2)}) collective-permute-start(f32[2,16,512]{2,1,0:T(8,128)} %own.1), channel_id=1, source_target_pairs={{0,63},{1,0},{2,1},{3,2},{4,3},{5,4},{6,5},{7,6},{8,7},{9,8},{10,9... | collective-permute-start | bytes 196616 | tf_op jit(solution)/shard_map/ppermute | solution.py:31
  21.2 28.3 %collective-permute-start.7 = (f32[2,16,512]{2,1,0:T(8,128)}, f32[2,16,512]{2,1,0:T(8,128)S(1)}, u32[]{:S(2)}, u32[]{:S(2)}) collective-permute-start(f32[2,16,512]{2,1,0:T(8,128)} %vown), channel_id=1, source_target_pairs={{0,63},{1,0},{2,1},{3,2},{4,3},{5,4},{6,5},{7,6},{8,7},{9,8},{10,9... | collective-permute-start | bytes 196616 | tf_op jit(solution)/shard_map/ppermute | solution.py:31
  24.7 24.8 %collective-permute-start.6 = (f32[2,16,512]{2,1,0:T(8,128)}, f32[2,16,512]{2,1,0:T(8,128)S(1)}, u32[]{:S(2)}, u32[]{:S(2)}) collective-permute-start(f32[2,16,512]{2,1,0:T(8,128)} %vown), channel_id=1, source_target_pairs={{0,1},{1,2},{2,3},{3,4},{4,5},{5,6},{6,7},{7,8},{8,9},{9,10},{10,1... | collective-permute-start | bytes 196616 | tf_op jit(solution)/shard_map/ppermute | solution.py:31
  24.7 0.8 copy-start
  25.6 18.5 %copy-start.1 = (f32[2,3,3,32,32]{4,3,2,1,0:T(8,128)S(1)}, f32[2,3,3,32,32]{4,3,2,1,0:T(8,128)}, u32[]{:S(2)}) copy-start(f32[2,3,3,32,32]{4,3,2,1,0:T(8,128)} %param.15) | copy-start | bytes 221188
  27.0 37.5 %all-to-all-start.3 = ((f32[64,1,128]{2,1,0:T(1,128)}), f32[64,1,128]{2,1,0:T(1,128)S(1)}, u32[]{:S(2)}, u32[]{:S(2)}) async-start(f32[64,1,128]{2,1,0:T(1,128)} %bitcast.3), calls=%async_computation.3 | async-start | bytes 65536 | tf_op jit(solution)/shard_map/all_to_all | solution.py:621
  45.9 0.7 copy-start.5
  46.7 0.7 copy-start.4
  48.8 0.7 copy-start.6
  48.8 0.7 copy-start.7
  49.5 0.7 copy-start.2
  49.5 0.7 copy-start.3

commit v6 on v4

--- a/solution.py
+++ b/solution.py
@@ -42,6 +42,10 @@
 
 def starts(first, count):
     return [min(first + BLOCK * i, first + count - BLOCK) for i in range(-(-count // BLOCK))]
+
+
+def blocks(first, count):
+    return [(s, first + BLOCK * i - s) for i, s in enumerate(starts(first, count))]
 
 
 def fold_lanes(x):
@@ -242,7 +246,7 @@
 def wide_conv(weights, high, low):
     x = jnp.concatenate([high, low, high], axis=0)
     y = jnp.dot(weights, x, preferred_element_type=F32)
-    return side_sum(y.reshape(BLOCK, 96, y.shape[1]))
+    return side_sum(y.reshape(-1, 96, y.shape[1]))
 
 
 def narrow_conv(weights, pair):
@@ -250,7 +254,7 @@
     high, low = halves(jnp.concatenate([turn(x, 1, 1), x, turn(x, -1, 1)], axis=0))
     x = jnp.concatenate([high, low, high], axis=0)
     y = jnp.dot(weights, x, preferred_element_type=F32)
-    return y.reshape(BLOCK, 32, y.shape[1])
+    return y.reshape(-1, 32, y.shape[1])
 
 
 def put(refs, at, value):
@@ -322,19 +326,19 @@
 
 def wide_terms(err, err_at, act, act_at, rows):
     total = None
-    lines = -(-rows // BLOCK)
-    for i in range(lines):
-        s = min(BLOCK * i, rows - BLOCK)
-        e = err[pl.ds((err_at + s) * 32, BLOCK * 32), :].reshape(BLOCK, 32, -1)
-        spent = BLOCK * i - s
-        if spent:
-            e = jnp.concatenate([jnp.zeros_like(e[:spent]), e[spent:]], axis=0)
-        high, low = halves(sided(e, 1).reshape(BLOCK * 96, -1))
+    for s, done in blocks(0, rows):
+        e = err[pl.ds((err_at + s + done) * 32, (BLOCK - done) * 32), :]
+        e = e.reshape(BLOCK - done, 32, -1)
+        high, low = halves(sided(e, 1).reshape((BLOCK - done) * 96, -1))
         ah, al = take(act, act_at + s - 1, SPAN)
         term = dot_nt(
             jnp.concatenate([high, high, low], axis=1), jnp.concatenate([ah, al, ah], axis=1)
         )
-        total = term if total is None else total + term
+        if done:
+            term = jnp.concatenate([total[: 96 * done], total[96 * done :] + term], axis=0)
+            total = term
+        else:
+            total = term if total is None else total + term
     total = total.reshape(BLOCK, 96, SPAN * 32)
     out = None
     for r in range(BLOCK):
@@ -413,30 +417,33 @@
     v = [jnp.concatenate([vprev[c, rows - 8 :], vown[c], vlater[c, :8]], axis=0) for c in range(2)]
     e3 = [step_size * item for item in adjoint]
 
-    def slope_of(act, at):
-        high, low = take(act, at, BLOCK)
+    def slope_of(act, at, count):
+        high, low = take(act, at, count)
         a = high.astype(F32) + low.astype(F32)
-        return (1.0 - a * a).reshape(BLOCK, 32, width)
+        return (1.0 - a * a).reshape(count, 32, width)
 
     def keep(ref, parts, at, value):
         put(parts, at, value)
-        ref[pl.ds(at * 32, BLOCK * 32), :] = value.reshape(BLOCK * 32, width)
+        ref[pl.ds(at * 32, value.shape[0] * 32), :] = value.reshape(value.shape[0] * 32, width)
 
     for copy in copies[:3]:
         copy.wait()
-    for s in starts(-3, rows + 6):
+    for s, done in blocks(-3, rows + 6):
         pair = [e3[c][s + 7 : s + 7 + SPAN] for c in range(2)]
-        keep(e2, split, s + 3, narrow_conv(band2[...], pair) * slope_of(a2, s + 3))
+        slope = slope_of(a2, s + 3 + done, BLOCK - done)
+        keep(e2, split, s + 3 + done, narrow_conv(band2[32 * done :, :], pair) * slope)
     for copy in copies[3:6]:
         copy.wait()
-    for s in starts(-2, rows + 4):
+    for s, done in blocks(-2, rows + 4):
         x = take(split, s + 2, SPAN)
-        keep(e1, other, s + 2, wide_conv(band1[...], *x) * slope_of(a1, s + 4))
+        slope = slope_of(a1, s + 4 + done, BLOCK - done)
+        keep(e1, other, s + 2 + done, wide_conv(band1[96 * done :, :], *x) * slope)
     for copy in copies[6:]:
         copy.wait()
-    for s in starts(-1, rows + 2):
+    for s, done in blocks(-1, rows + 2):
         x = take(other, s + 1, SPAN)
-        keep(e0, split, s + 1, wide_conv(band0[...], *x) * slope_of(a0, s + 5))
+        slope = slope_of(a0, s + 5 + done, BLOCK - done)
+        keep(e0, split, s + 1 + done, wide_conv(band0[96 * done :, :], *x) * slope)
 
     own = slice(8, 8 + rows)
     cells = (rows + 2) * 32

time: 142 us -> 141 us (level)
  no operation moved by 1% of the time
where the time goes in v6:
time: 141 us; the launch traced here: 140 us
  blocking collectives  60.3 us (43%)
  starting transfers between devices  39.8 us (28%)
  Pallas kernels  24 us (17%)
  waiting for transfers between devices  6.39 us (5%)
  local copies, waits for them, and re-layouts  6.24 us (4%)
  other arithmetic  2.08 us (1%)
  between operations  1.46 us (1%)
    all_to_all x2, blocking collectives, from_everyone(): lax.all_to_all(jnp.broadcast_to(x[None], (length, *x.shape)), axis, 0, 0,...  50.1 us
    ppermute x4, starting transfers between devices, shifted(): return lax.ppermute(value, axis, pairs)  24.1 us
    all_to_all x1, starting transfers between devices, body(): lax.all_to_all(sums.reshape(members, 1, 128), GX, 0, 0, tiled=True)  15.7 us
    pallas_call x1, Pallas kernels, body(): call(backward_kernel, (shape_of(2, rows, width), shape_of(192, 128)), [pl...  12 us
    all_to_all x1, blocking collectives, total_of(): part = lax.all_to_all(part, local, 0, 0, tiled=True).sum(axis=0)  10.2 us
    pallas_call x1, Pallas kernels, body(): call(forward_kernel, tuple(held), [pltpu.VMEM(item.shape, item.dtype) for...  7.88 us
    all_to_all x1, waiting for transfers between devices, body(): lax.all_to_all(sums.reshape(members, 1, 128), GX, 0, 0, tiled=True)  6.38 us
  transfers between devices with their start and end apart: 5, of which 1 were waited for; matrix products, arithmetic and copies ran while one was open for 4% of the time, Pallas kernels for 7%

profile of v6, /device:TPU:37, one launch (start us, length us, event | category | flops | bytes accessed | tf_op | source)
XLA Modules:
  0.0 140.5 jit_solution(6255851152298136042)
XLA Ops:
  0.6 3.2 %collective-permute-start.4 = (f32[2,16,512]{2,1,0:T(8,128)}, f32[2,16,512]{2,1,0:T(8,128)S(1)}, u32[]{:S(2)}, u32[]{:S(2)}) collective-permute-start(f32[2,16,512]{2,1,0:T(8,128)} %own.1), channel_id=1, source_target_pairs={{0,1},{1,2},{2,3},{3,4},{4,5},{5,6},{6,7},{7,8},{8,9},{9,10},{10,1... | collective-permute-start | bytes 196616 | tf_op jit(solution)/shard_map/ppermute | solution.py:31
  3.8 17.3 %collective-permute-start.5 = (f32[2,16,512]{2,1,0:T(8,128)}, f32[2,16,512]{2,1,0:T(8,128)S(1)}, u32[]{:S(2)}, u32[]{:S(2)}) collective-permute-start(f32[2,16,512]{2,1,0:T(8,128)} %own.1), channel_id=1, source_target_pairs={{0,63},{1,0},{2,1},{3,2},{4,3},{5,4},{6,5},{7,6},{8,7},{9,8},{10,9... | collective-permute-start | bytes 196616 | tf_op jit(solution)/shard_map/ppermute | solution.py:31
  21.2 3.6 %collective-permute-start.7 = (f32[2,16,512]{2,1,0:T(8,128)}, f32[2,16,512]{2,1,0:T(8,128)S(1)}, u32[]{:S(2)}, u32[]{:S(2)}) collective-permute-start(f32[2,16,512]{2,1,0:T(8,128)} %vown), channel_id=1, source_target_pairs={{0,63},{1,0},{2,1},{3,2},{4,3},{5,4},{6,5},{7,6},{8,7},{9,8},{10,9... | collective-permute-start | bytes 196616 | tf_op jit(solution)/shard_map/ppermute | solution.py:31
  24.7 0.8 copy-done
  25.6 1.4 %shard_map.126 = (f32[8,32,512]{2,1,0:T(8,128)S(1)}, f32[64,128]{1,0:T(8,128)}, f32[2,32,512]{2,1,0:T(8,128)S(1)}) custom-call(f32[2,16,512]{2,1,0:T(8,128)S(1)} %collective-permute-done.4.prev, f32[2,16,512]{2,1,0:T(8,128)S(1)} %copy-done, f32[2,16,512]{2,1,0:T(8,128)S(1)} %collective-permute-done.5.later), custom_call_target="tpu_custom_call" | custom-call | tf_op jit(solution)/shard_map/pallas_call | solution.py:598
  27.0 15.7 %all-to-all-start.3 = ((f32[64,1,128]{2,1,0:T(1,128)}), f32[64,1,128]{2,1,0:T(1,128)S(1)}, u32[]{:S(2)}, u32[]{:S(2)}) async-start(f32[64,1,128]{2,1,0:T(1,128)} %bitcast.3), calls=%async_computation.3 | async-start | bytes 65536 | tf_op jit(solution)/shard_map/all_to_all | solution.py:607
  42.7 0.7 reverse_bitcast_fusion.2
  43.4 0.7 pad_maximum_fusion.3.out_taps
  45.2 0.7 pad_maximum_fusion.2.wide_back
  45.9 0.7 copy-done.5
  46.7 0.6 pad.36.narrow_back
  47.5 0.6 pad.32.narrow
  48.1 0.7 pad_maximum_fusion.1.wide
  48.8 0.7 copy-done.6
  49.5 0.7 broadcast_in_dim.15.bias
  50.3 7.9 %shard_map.128 = (bf16[832,512]{1,0:T(8,128)(2,1)}, bf16[832,512]{1,0:T(8,128)(2,1)}, bf16[768,512]{1,0:T(8,128)(2,1)}, bf16[768,512]{1,0:T(8,128)(2,1)}, bf16[7...) custom-call(f32[2,16,512]{2,1,0:T(8,128)} %copy-done.3, ...), custom_call_target="tpu_custom_call" | custom-call | tf_op jit(solution)/shard_map/pallas_call | solution.py:629
  58.1 6.4 %all-to-all-done.3 = f32[64,1,128]{2,1,0:T(1,128)S(1)} async-done(((f32[64,1,128]{2,1,0:T(1,128)}), f32[64,1,128]{2,1,0:T(1,128)S(1)}, u32[]{:S(2)}, u32[]{:S(2)}) %all-to-all-start.3) | async-done | bytes 32800 | tf_op jit(solution)/shard_map/all_to_all | solution.py:607
  64.5 1.0 shard_map.127
  66.2 0.2 conditional.1
  66.4 12.0 %shard_map.129 = (f32[2,16,512]{2,1,0:T(8,128)}, f32[192,128]{1,0:T(8,128)}) custom-call(f32[1,1]{1,0:T(1,128)} %constant.5.clone.1.factor, f32[32,512]{1,0:T(8,128)S(1)} %get-tuple-element.229.pressure, f32[2,32,512]{2,1,0:T(8,128)S(1)} %get-tuple-element.71.around, f32[2,16,512]{2,1,0:T(8,128)} %copy-done.3, f32[2,16,512]{2,1,0:T(8,128)} %vown, ...), custom_call_target="tpu_custom_call" | custom-call | tf_op jit(solution)/shard_map/pallas_call | solution.py:656
  78.4 10.2 %all_to_all.38 = f32[8,24,128]{2,1,0:T(8,128)S(1)} all-to-all(f32[8,24,128]{2,1,0:T(8,128)} %bitcast.50), channel_id=1, replica_groups=mesh['groups'=4,'gx_far'=8,'gx_near'=4,'gx_core'=2] {'gx_near','gx_core'}, dimensions={0} | all-to-all | bytes 196608 | tf_op jit(solution)/shard_map/all_to_all | solution.py:550
  88.6 36.8 %all_to_all.39 = f32[8,24,128]{2,1,0:T(8,128)S(1)} all-to-all(f32[8,24,128]{2,1,0:T(8,128)S(1)} %broadcast_in_dim.16), channel_id=1, replica_groups=mesh['groups'=4,'gx_far'=8,'gx_near'=4,'gx_core'=2] {'gx_far'}, dimensions={0} | all-to-all | bytes 196608 | tf_op jit(solution)/shard_map/all_to_all | solution.py:25
  125.5 13.3 %all_to_all.40 = f32[8,24,128]{2,1,0:T(8,128)} all-to-all(f32[8,24,128]{2,1,0:T(8,128)S(1)} %broadcast_in_dim.17), channel_id=1, replica_groups=mesh['groups'=4,'gx_far'=8,'gx_near'=4,'gx_core'=2] {'gx_near','gx_core'}, dimensions={0} | all-to-all | bytes 196608 | tf_op jit(solution)/shard_map/all_to_all | solution.py:25
  138.7 1.7 %shard_map.130 = (f32[3,3,2,32]{3,2,1,0:T(2,128)}, f32[1,32]{1,0:T(1,128)}, f32[2,3,3,32,32]{4,3,2,1,0:T(8,128)}, f32[2,32]{1,0:T(2,128)}, f32[3,3,2,32]{3,2,1,0:T(2,128)}, /*index=5*/f32[1,2]{1,0:T(1,128)}) custom-call(f32[192,128]{1,0:T(8,128)} %bitcast.49), custom_call_target="tpu_custom_call" | custom-call | tf_op jit(solution)/shard_map/pallas_call | solution.py:674
  (45 shorter events, 1.5 us)
Async XLA Ops:
  0.6 24.1 %collective-permute-start.4 = (f32[2,16,512]{2,1,0:T(8,128)}, f32[2,16,512]{2,1,0:T(8,128)S(1)}, u32[]{:S(2)}, u32[]{:S(2)}) collective-permute-start(f32[2,16,512]{2,1,0:T(8,128)} %own.1), channel_id=1, source_target_pairs={{0,1},{1,2},{2,3},{3,4},{4,5},{5,6},{6,7},{7,8},{8,9},{9,10},{10,1... | collective-permute-start | bytes 196616 | tf_op jit(solution)/shard_map/ppermute | solution.py:31
  3.8 20.9 %collective-permute-start.5 = (f32[2,16,512]{2,1,0:T(8,128)}, f32[2,16,512]{2,1,0:T(8,128)S(1)}, u32[]{:S(2)}, u32[]{:S(2)}) collective-permute-start(f32[2,16,512]{2,1,0:T(8,128)} %own.1), channel_id=1, source_target_pairs={{0,63},{1,0},{2,1},{3,2},{4,3},{5,4},{6,5},{7,6},{8,7},{9,8},{10,9... | collective-permute-start | bytes 196616 | tf_op jit(solution)/shard_map/ppermute | solution.py:31
  21.2 28.3 %collective-permute-start.7 = (f32[2,16,512]{2,1,0:T(8,128)}, f32[2,16,512]{2,1,0:T(8,128)S(1)}, u32[]{:S(2)}, u32[]{:S(2)}) collective-permute-start(f32[2,16,512]{2,1,0:T(8,128)} %vown), channel_id=1, source_target_pairs={{0,63},{1,0},{2,1},{3,2},{4,3},{5,4},{6,5},{7,6},{8,7},{9,8},{10,9... | collective-permute-start | bytes 196616 | tf_op jit(solution)/shard_map/ppermute | solution.py:31
  24.7 24.8 %collective-permute-start.6 = (f32[2,16,512]{2,1,0:T(8,128)}, f32[2,16,512]{2,1,0:T(8,128)S(1)}, u32[]{:S(2)}, u32[]{:S(2)}) collective-permute-start(f32[2,16,512]{2,1,0:T(8,128)} %vown), channel_id=1, source_target_pairs={{0,1},{1,2},{2,3},{3,4},{4,5},{5,6},{6,7},{7,8},{8,9},{9,10},{10,1... | collective-permute-start | bytes 196616 | tf_op jit(solution)/shard_map/ppermute | solution.py:31
  24.7 0.8 copy-start
  25.6 18.5 %copy-start.1 = (f32[2,3,3,32,32]{4,3,2,1,0:T(8,128)S(1)}, f32[2,3,3,32,32]{4,3,2,1,0:T(8,128)}, u32[]{:S(2)}) copy-start(f32[2,3,3,32,32]{4,3,2,1,0:T(8,128)} %param.15) | copy-start | bytes 221188
  27.0 37.5 %all-to-all-start.3 = ((f32[64,1,128]{2,1,0:T(1,128)}), f32[64,1,128]{2,1,0:T(1,128)S(1)}, u32[]{:S(2)}, u32[]{:S(2)}) async-start(f32[64,1,128]{2,1,0:T(1,128)} %bitcast.3), calls=%async_computation.3 | async-start | bytes 65536 | tf_op jit(solution)/shard_map/all_to_all | solution.py:607
  45.9 0.7 copy-start.5
  46.7 0.7 copy-start.4
  48.8 0.7 copy-start.6
  48.8 0.7 copy-start.7
  49.5 0.7 copy-start.2
  49.5 0.7 copy-start.3
